TPU v7x, 32 devices: a whole 2x2x4 slice. The times are simulated.
32 devices in a mesh: ta: 4 (over z), sa: 8 (over y, x, core).
Axes of the slice: x: 2, y: 2, z: 4, core: 2. Of those that a mesh axis runs over, the one named last changes fastest.
Arguments:
- frames: float32 [16, 8, 512, 4096], P('ta', 'sa'), may hold values from -6 to 6
- taps: float32 [7], replicated, may hold values from 0.1 to 0.3
Outputs:
- columns: float32 [64, 16, 512, 512], P('sa', 'ta')
All inputs are finite; a program needn't handle non-finite values.
Results may differ from a plain program's by a relative error of at most 0.00002.
Values sent between devices are 32-bit elements; how exact they have to be, the bound alone decides.
No kernel may reach another device: no remote copies, remote signals or barrier semaphores. Data moves between devices by JAX's collectives and lax.ppermute only.
A program may use at most 256 MiB of HBM per device.

v0:
```python
import jax
import jax.numpy as jnp
from jax import lax
from jax.sharding import PartitionSpec as P

TS = 512


def extended_2(cells, sides, width):
    for axis, dim in sides:
        count = lax.axis_size(axis)
        ends = count - 1
        head = lax.slice_in_dim(cells, 0, width, axis=dim)
        tail = lax.slice_in_dim(cells, cells.shape[dim] - width, cells.shape[dim], axis=dim)
        cells = jnp.concatenate(
            [
                lax.ppermute(tail, axis, [(i, (i + 1) % count) for i in range(ends)]),
                cells,
                lax.ppermute(head, axis, [((i + 1) % count, i) for i in range(ends)]),
            ],
            axis=dim,
        )
    return cells


def pack_tiles(block, readers):
    count = block.shape[0]
    per_tile = TS // readers
    tile_rows = block.shape[2] // per_tile
    tile_cols = block.shape[3] // TS
    shaped = block.reshape(count, tile_rows, per_tile, tile_cols, TS)
    return shaped.transpose(1, 3, 0, 2, 4).reshape(tile_rows * tile_cols, 1, count, per_tile, TS)


def unpack_tiles(received):
    owned = received.shape[0]
    count = received.shape[2]
    return received.transpose(0, 2, 3, 1, 4).reshape(owned, count, TS, TS)


def on_device(frames, taps):
    steps = frames.shape[0]
    readers = lax.axis_size("sa")
    received = lax.all_to_all(
        pack_tiles(frames, readers), "sa", split_axis=0, concat_axis=1, tiled=True
    )
    tiles = unpack_tiles(received)
    extended = extended_2(tiles, (("ta", 1),), 3)
    total = jnp.zeros((extended.shape[0], steps, TS, TS), jnp.float32)
    for offset in range(7):
        total = total + taps[offset] * extended[:, offset : offset + steps]
    return total


def solution(mesh):
    placed = (P("ta", "sa", None, None), P())
    return jax.shard_map(
        on_device, mesh=mesh, in_specs=placed, out_specs=P("sa", "ta", None, None), check_vma=False
    )
```

profile of v0, /device:TPU:0, one launch (start us, length us, event | category | flops | bytes accessed | tf_op | source)
XLA Modules:
  0.0 1142.3 jit_solution(14448742951515873485)
XLA Ops:
  0.0 38.0 %copy.8 = f32[256,8,8,512]{3,2,1,0:T(8,128)} copy(f32[256,8,8,512]{3,1,2,0:T(8,128)} %bitcast.32) | data formatting | bytes 67108864
  38.0 28.2 %copy.5 = f32[8,8,4,64,512]{4,3,2,1,0:T(8,128)S(1)} copy(f32[8,8,4,64,512]{4,1,3,0,2:T(8,128)} %bitcast.31) | data formatting | bytes 67108864 | tf_op jit(solution)/shard_map/transpose | solution.py:32
  66.3 369.0 %all_to_all.18 = f32[64,1,4,64,512]{4,3,2,1,0:T(8,128)} all-to-all(f32[64,1,4,64,512]{4,3,2,1,0:T(8,128)S(1)} %bitcast.29), channel_id=1, replica_groups=mesh['ta'=4,'sa'=8] {'sa'}, dimensions={0} | all-to-all | bytes 67108864 | tf_op jit(solution)/shard_map/all_to_all | solution.py:44
  435.2 31.8 %copy.10 = f32[8,4,64,8,512]{4,3,2,1,0:T(8,128)} copy(f32[8,4,64,8,512]{4,2,1,0,3:T(8,128)} %bitcast.30) | data formatting | bytes 67108864 | tf_op jit(solution)/shard_map/transpose | solution.py:38
  467.0 0.0 copy-start
  467.0 32.0 %fusion.16 = (f32[8,3,512,512]{3,2,1,0:T(8,128)}, f32[8,3,512,512]{3,2,1,0:T(8,128)}) fusion(f32[8,4,512,512]{3,2,1,0:T(8,128)} %bitcast.27), kind=kLoop, calls=%fused_computation.27 | loop fusion | bytes 100663296 | tf_op jit(solution)/shard_map/slice | solution.py:14
  498.9 12.5 %collective-permute-start = (f32[8,3,512,512]{3,2,1,0:T(8,128)}, f32[8,3,512,512]{3,2,1,0:T(8,128)}, u32[]{:S(2)}, u32[]{:S(2)}) collective-permute-start(f32[8,3,512,512]{3,2,1,0:T(8,128)} %get-tuple-element.5), channel_id=1, source_target_pairs={{0,8},{8,16},{16,24},{1,9},{9,17},{17,25},{2,10},{10,18},{18,26},{... | collective-permute-start | bytes 75497480 | tf_op jit(solution)/shard_map/ppermute | solution.py:17
  511.4 1.3 collective-permute-start.1
  512.7 0.0 copy-done
  512.7 0.7 fusion.17
  513.4 528.7 %collective-permute-done = f32[8,3,512,512]{3,2,1,0:T(8,128)} collective-permute-done((f32[8,3,512,512]{3,2,1,0:T(8,128)}, f32[8,3,512,512]{3,2,1,0:T(8,128)}, u32[]{:S(2)}, u32[]{:S(2)}) %collective-permute-start) | collective-permute-done | bytes 25165856 | tf_op jit(solution)/shard_map/ppermute | solution.py:17
  1042.1 12.4 %collective-permute-done.1 = f32[8,3,512,512]{3,2,1,0:T(8,128)} collective-permute-done((f32[8,3,512,512]{3,2,1,0:T(8,128)}, f32[8,3,512,512]{3,2,1,0:T(8,128)}, u32[]{:S(2)}, u32[]{:S(2)}) %collective-permute-start.1) | collective-permute-done | bytes 25165856 | tf_op jit(solution)/shard_map/ppermute | solution.py:19
  1054.5 87.8 %fusion.3 = f32[8,4,512,512]{3,2,1,0:T(8,128)} fusion(f32[8,4,512,512]{3,2,1,0:T(8,128)} %bitcast.28, f32[8,3,512,512]{3,2,1,0:T(8,128)} %collective-permute-done.1, f32[8,3,512,512]{3,2,1,0:T(8,128)} %collective-permute-done, f32[]{:T(128)} %bitcast.14, f32[]{:T(128)} %bitcast.13, f32[]{:T(128)} %bitcast.12, f32[]{:T(128)} %bitcast.11, f32[]{:T(128)} %bitcast.10, ...), kind=kLoop, calls=%fused_computation.11 | loop fusion | flops 159383552 | bytes 117440544 | tf_op jit(solution)/shard_map/add | solution.py:51
Async XLA Ops:
  467.0 45.7 %copy-start = (f32[7]{0:T(128)S(1)}, f32[7]{0:T(128)}, u32[]{:S(2)}) copy-start(f32[7]{0:T(128)} %param.3) | copy-start | bytes 88
  498.9 543.1 %collective-permute-start = (f32[8,3,512,512]{3,2,1,0:T(8,128)}, f32[8,3,512,512]{3,2,1,0:T(8,128)}, u32[]{:S(2)}, u32[]{:S(2)}) collective-permute-start(f32[8,3,512,512]{3,2,1,0:T(8,128)} %get-tuple-element.5), channel_id=1, source_target_pairs={{0,8},{8,16},{16,24},{1,9},{9,17},{17,25},{2,10},{10,18},{18,26},{... | collective-permute-start | bytes 75497480 | tf_op jit(solution)/shard_map/ppermute | solution.py:17
  511.4 543.1 %collective-permute-start.1 = (f32[8,3,512,512]{3,2,1,0:T(8,128)}, f32[8,3,512,512]{3,2,1,0:T(8,128)}, u32[]{:S(2)}, u32[]{:S(2)}) collective-permute-start(f32[8,3,512,512]{3,2,1,0:T(8,128)} %get-tuple-element.6), channel_id=1, source_target_pairs={{8,0},{16,8},{24,16},{9,1},{17,9},{25,17},{10,2},{18,10},{26,18},{... | collective-permute-start | bytes 75497480 | tf_op jit(solution)/shard_map/ppermute | solution.py:19
where the time goes:
time: 1140 us
  waiting for transfers between devices  541 us (47%)
  blocking collectives  369 us (32%)
  local copies, waits for them, and re-layouts  131 us (11%)
  other arithmetic  87.8 us (8%)
  starting transfers between devices  13.7 us (1%)
    ppermute x1, waiting for transfers between devices, extended_2(): lax.ppermute(tail, axis, [(i, (i + 1) % count) for i in range(ends)])  529 us
    all_to_all x1, blocking collectives, on_device(): lax.all_to_all(pack_tiles(frames, readers), 'sa', split_axis=0, concat_ax...  369 us
    add x1, other arithmetic, on_device(): total = total + taps[offset] * extended[:, offset:offset + steps]  87.8 us
    unnamed x3, local copies, waits for them, and re-layouts  38 us
    slice x1, local copies, waits for them, and re-layouts, extended_2(): lax.slice_in_dim(cells, cells.shape[dim] - width, cells.shape[dim], axis=...  32 us
    transpose x1, local copies, waits for them, and re-layouts, unpack_tiles(): return received.transpose(0, 2, 3, 1, 4).reshape(owned, count, TS, TS)  31.8 us
    transpose x1, local copies, waits for them, and re-layouts, pack_tiles(): shaped.transpose(1, 3, 0, 2, 4)  28.2 us
  transfers between devices with their start and end apart: 2, of which 2 were waited for; matrix products, arithmetic and copies ran while one was open for 0% of the time, Pallas kernels for 0%

commit v1 on v0

v1 whole, which is shorter than its diff:
```python
import functools
import math

import jax
import jax.numpy as jnp
from jax import lax
from jax.experimental import pallas as pl
from jax.experimental.pallas import tpu as pltpu
from jax.sharding import PartitionSpec as P


TS = 512
REACH = 3
LANES = 128
SUBLANES = 8
SHARES = (2, 3, 4, 5, 6, 6, 4, 2)


def chunk_bounds(width):
    units = width // LANES
    edges, seen = [0], 0
    for share in SHARES:
        seen += share
        edge = units * seen // sum(SHARES)
        if edge > edges[-1]:
            edges.append(edge)
    return [(a * LANES, b * LANES) for a, b in zip(edges, edges[1:])]


def pack_kernel(per_tile, frames_ref, first_ref, middle_ref, last_ref):
    steps = frames_ref.shape[0]
    for tile in range(first_ref.shape[0]):
        rows = pl.ds(tile * per_tile, per_tile)
        first_ref[tile, 0, 0] = frames_ref[0, 0, rows, :]
        for t in range(1, steps - 1):
            middle_ref[tile, 0, t - 1] = frames_ref[t, 0, rows, :]
        last_ref[tile, 0, 0] = frames_ref[steps - 1, 0, rows, :]


def pack_chunk(frames, readers, per_tile, span, start, width):
    steps, _, strip, columns = frames.shape
    tile_rows, groups = strip // per_tile, columns // span
    block = math.gcd(start, width)
    block = math.gcd(block, span) if groups > 1 else block

    def piece(depth):
        shape = (tile_rows, groups, depth, per_tile, width)
        spec = pl.BlockSpec(
            (tile_rows, 1, depth, per_tile, block), lambda g, i: (0, g, 0, 0, i)
        )
        return jax.ShapeDtypeStruct(shape, jnp.float32), spec

    pieces = [piece(1), piece(steps - 2), piece(1)]
    outs = pl.pallas_call(
        functools.partial(pack_kernel, per_tile),
        grid=(groups, width // block),
        out_shape=[p[0] for p in pieces],
        in_specs=[
            pl.BlockSpec(
                (steps, 1, strip, block),
                lambda g, i: (0, 0, 0, g * (span // block) + start // block + i),
            )
        ],
        out_specs=[p[1] for p in pieces],
        cost_estimate=pl.CostEstimate(
            flops=steps * strip * width * groups,
            bytes_accessed=8 * steps * strip * width * groups,
            transcendentals=0,
        ),
        name="pack",
    )(frames)
    return [o.reshape((readers,) + o.shape[2:]) for o in outs]


def smooth_kernel(readers, groups, taps_ref, *refs):
    first, middle, last, before_mid, before_last, after_first, after_mid = refs[:7]
    out_ref = refs[-1]
    steps = out_ref.shape[1]
    taps = [taps_ref[j] for j in range(2 * REACH + 1)]

    def body(group, carry):
        rows = pl.ds(pl.multiple_of(group * SUBLANES, SUBLANES), SUBLANES)
        for s in range(readers):
            field = [
                before_mid[s, 0, rows, :],
                before_mid[s, 1, rows, :],
                before_last[s, 0, rows, :],
                first[s, 0, rows, :],
                middle[s, 0, rows, :],
                middle[s, 1, rows, :],
                last[s, 0, rows, :],
                after_first[s, 0, rows, :],
                after_mid[s, 0, rows, :],
                after_mid[s, 1, rows, :],
            ]
            for t in range(steps):
                total = taps[0] * field[t]
                for j in range(1, 2 * REACH + 1):
                    total = total + taps[j] * field[t + j]
                at = group * (SUBLANES * readers) + s
                out_ref[0, t, pl.ds(at, SUBLANES, stride=readers), :] = total
        return carry

    lax.fori_loop(0, groups, body, 0)


def smooth_chunk(taps, pieces, out, out_shape, start, width):
    readers, _, per_tile, _ = pieces[0].shape
    steps = out_shape[1]
    offset = start // LANES
    per_row = TS // LANES

    def piece_spec(piece):
        return pl.BlockSpec(
            (readers, piece.shape[1], per_tile, LANES), lambda i: (0, 0, 0, i)
        )

    in_specs = [pl.BlockSpec(memory_space=pltpu.SMEM)] + [piece_spec(p) for p in pieces]
    operands = [taps, *pieces]
    aliases = {}
    if out is not None:
        in_specs.append(pl.BlockSpec(memory_space=pl.ANY))
        aliases = {len(operands): 0}
        operands.append(out)
    elements = readers * per_tile * width
    return pl.pallas_call(
        functools.partial(smooth_kernel, readers, per_tile // SUBLANES),
        grid=(width // LANES,),
        out_shape=jax.ShapeDtypeStruct(out_shape, jnp.float32),
        in_specs=in_specs,
        out_specs=pl.BlockSpec(
            (1, steps, TS, LANES),
            lambda i: ((i + offset) // per_row, 0, 0, (i + offset) % per_row),
        ),
        input_output_aliases=aliases,
        cost_estimate=pl.CostEstimate(
            flops=14 * steps * elements, bytes_accessed=14 * 4 * elements, transcendentals=0
        ),
        compiler_params=pltpu.CompilerParams(dimension_semantics=("arbitrary",)),
        name="smooth",
    )(*operands)


def on_device(frames, taps):
    steps, _, strip, columns = frames.shape
    readers = lax.axis_size("sa")
    count = lax.axis_size("ta")
    per_tile = TS // readers
    tile_rows = strip // per_tile
    owned = tile_rows * (columns // TS) // readers
    span = owned * TS
    out_shape = (owned, steps, TS, TS)
    up = [(i, i + 1) for i in range(count - 1)]
    down = [(i + 1, i) for i in range(count - 1)]
    swap = functools.partial(
        lax.all_to_all, axis_name="sa", split_axis=0, concat_axis=0, tiled=True
    )

    out = None
    for start, stop in chunk_bounds(span):
        first, middle, last = pack_chunk(frames, readers, per_tile, span, start, stop - start)
        middle = swap(middle)
        before_mid = lax.ppermute(middle, "ta", up)
        after_mid = lax.ppermute(middle, "ta", down)
        first = swap(first)
        after_first = lax.ppermute(first, "ta", down)
        last = swap(last)
        before_last = lax.ppermute(last, "ta", up)
        pieces = (first, middle, last, before_mid, before_last, after_first, after_mid)
        out = smooth_chunk(taps, pieces, out, out_shape, start, stop - start)
    return out


def solution(mesh):
    placed = (P("ta", "sa", None, None), P())

    return jax.shard_map(
        on_device, mesh=mesh, in_specs=placed, out_specs=P("sa", "ta", None, None), check_vma=False
    )
```

time: 1140 us -> 966 us (0.85)
  starting transfers between devices: 13.7 us -> 145 us
  local copies, waits for them, and re-layouts: 131 us -> 6.61 us
  blocking collectives: 369 us -> 264 us
  Pallas kernels: 0 us -> 97.1 us
  waiting for transfers between devices: 541 us -> 448 us
  other arithmetic: 87.8 us -> 0 us
    ppermute x2 -> x32, waiting for transfers between devices: 541 us -> 363 us  [the longest x8 197 us: on_device(): before_mid = lax.ppermute(middle, 'ta', up)]
    all_to_all x1 -> x12, blocking collectives: 369 us -> 264 us  [the longest x7 143 us: on_device(): last = swap(last)]
    pallas_call x0 -> x16, Pallas kernels: none -> 97.1 us  [the longest x8 58.7 us: smooth_chunk(): pl.pallas_call(functools.partial(smooth_kernel, readers, per_tile // SUBL...]
    add x1 -> x0, other arithmetic: 87.8 us -> none  [on_device(): total = total + taps[offset] * extended[:, offset:offset + steps]]
    ppermute x2 -> x32, starting transfers between devices: 13.7 us -> 99.4 us  [the longest x8 42.5 us: on_device(): before_mid = lax.ppermute(middle, 'ta', up)]
    all_to_all x0 -> x12, waiting for transfers between devices: none -> 85.6 us  [the longest x6 45.7 us: on_device(): middle = swap(middle)]
    transpose x2 -> x0, local copies, waits for them, and re-layouts: 60 us -> none  [the longest x1 31.8 us: unpack_tiles(): return received.transpose(0, 2, 3, 1, 4).reshape(owned, count, TS, TS)]
    all_to_all x0 -> x12, starting transfers between devices: none -> 45.6 us  [the longest x6 23.1 us: on_device(): middle = swap(middle)]
  transfers between devices with their start and end apart: 2 -> 44, of which waited for: 2 -> 25; matrix products, arithmetic and copies ran while one was open for 0% -> 0% of each run, Pallas kernels for 0% -> 9%
where the time goes in v1:
time: 966 us; the launch traced here: 962 us
  waiting for transfers between devices  448 us (46%)
  blocking collectives  264 us (27%)
  starting transfers between devices  145 us (15%)
  Pallas kernels  97.1 us (10%)
    ppermute x8, waiting for transfers between devices, on_device(): before_mid = lax.ppermute(middle, 'ta', up)  197 us
    all_to_all x7, blocking collectives, on_device(): last = swap(last)  143 us
    ppermute x8, waiting for transfers between devices, on_device(): before_last = lax.ppermute(last, 'ta', up)  84.5 us
    all_to_all x3, blocking collectives, on_device(): first = swap(first)  62.3 us
    all_to_all x2, blocking collectives, on_device(): middle = swap(middle)  59.6 us
    pallas_call x8, Pallas kernels, smooth_chunk(): pl.pallas_call(functools.partial(smooth_kernel, readers, per_tile // SUBL...  58.7 us
    ppermute x8, waiting for transfers between devices, on_device(): after_first = lax.ppermute(first, 'ta', down)  49 us
    all_to_all x6, waiting for transfers between devices, on_device(): middle = swap(middle)  45.7 us
  transfers between devices with their start and end apart: 44, of which 25 were waited for; matrix products, arithmetic and copies ran while one was open for 0% of the time, Pallas kernels for 9%

profile of v1, /device:TPU:0, one launch (start us, length us, event | category | flops | bytes accessed | tf_op | source)
XLA Modules:
  0.0 962.1 jit_solution(6038222044417028710)
XLA Ops:
  3.0 14.9 %all_to_all.120.refs_2_ = f32[8,1,64,256]{3,2,1,0:T(8,128)S(1)} all-to-all(f32[8,1,64,256]{3,2,1,0:T(8,128)} %bitcast.44), channel_id=1, replica_groups=mesh['ta'=4,'sa'=8] {'sa'}, dimensions={0} | all-to-all | bytes 1048576 | tf_op jit(solution)/shard_map/all_to_all | solution.py:167
  21.4 4.4 pack.14
  25.8 5.2 all-to-all-done.21.refs_0_
  31.0 16.7 %all_to_all.121.refs_2_ = f32[8,1,64,384]{3,2,1,0:T(8,128)} all-to-all(f32[8,1,64,384]{3,2,1,0:T(8,128)} %bitcast.40), channel_id=1, replica_groups=mesh['ta'=4,'sa'=8] {'sa'}, dimensions={0} | all-to-all | bytes 1572864 | tf_op jit(solution)/shard_map/all_to_all | solution.py:167
  47.7 15.6 %all_to_all.122.refs_0_ = f32[8,1,64,384]{3,2,1,0:T(8,128)} all-to-all(f32[8,1,64,384]{3,2,1,0:T(8,128)S(1)} %bitcast.39), channel_id=1, replica_groups=mesh['ta'=4,'sa'=8] {'sa'}, dimensions={0} | all-to-all | bytes 1572864 | tf_op jit(solution)/shard_map/all_to_all | solution.py:165
  66.9 4.7 pack.13
  71.7 10.6 %all-to-all-done.22.refs_1_ = f32[8,2,64,256]{3,2,1,0:T(8,128)S(1)} async-done(((f32[8,2,64,256]{3,2,1,0:T(8,128)}), f32[8,2,64,256]{3,2,1,0:T(8,128)S(1)}, u32[]{:S(2)}, u32[]{:S(2)}) %all-to-all-start.22) | async-done | bytes 1048608 | tf_op jit(solution)/shard_map/all_to_all | solution.py:162
  82.2 19.5 %all_to_all.123.refs_2_ = f32[8,1,64,512]{3,2,1,0:T(8,128)} all-to-all(f32[8,1,64,512]{3,2,1,0:T(8,128)} %bitcast.37), channel_id=1, replica_groups=mesh['ta'=4,'sa'=8] {'sa'}, dimensions={0} | all-to-all | bytes 2097152 | tf_op jit(solution)/shard_map/all_to_all | solution.py:167
  109.1 11.6 %all-to-all-done.15.refs_0_ = f32[8,1,64,512]{3,2,1,0:T(8,128)S(1)} async-done(((f32[8,1,64,512]{3,2,1,0:T(8,128)}), f32[8,1,64,512]{3,2,1,0:T(8,128)S(1)}, u32[]{:S(2)}, u32[]{:S(2)}) %all-to-all-start.15) | async-done | bytes 1048608 | tf_op jit(solution)/shard_map/all_to_all | solution.py:165
  120.7 19.6 %all_to_all.124.refs_2_ = f32[8,1,64,512]{3,2,1,0:T(8,128)} all-to-all(f32[8,1,64,512]{3,2,1,0:T(8,128)} %bitcast.38), channel_id=1, replica_groups=mesh['ta'=4,'sa'=8] {'sa'}, dimensions={0} | all-to-all | bytes 2097152 | tf_op jit(solution)/shard_map/all_to_all | solution.py:167
  143.8 6.6 pack.12
  150.4 8.8 all-to-all-done.3.refs_0_
  159.1 22.4 %all_to_all.125.refs_2_ = f32[8,1,64,640]{3,2,1,0:T(8,128)} all-to-all(f32[8,1,64,640]{3,2,1,0:T(8,128)} %bitcast.35), channel_id=1, replica_groups=mesh['ta'=4,'sa'=8] {'sa'}, dimensions={0} | all-to-all | bytes 2621440 | tf_op jit(solution)/shard_map/all_to_all | solution.py:167
  181.5 21.3 %all_to_all.126.refs_0_ = f32[8,1,64,640]{3,2,1,0:T(8,128)} all-to-all(f32[8,1,64,640]{3,2,1,0:T(8,128)S(1)} %bitcast.34), channel_id=1, replica_groups=mesh['ta'=4,'sa'=8] {'sa'}, dimensions={0} | all-to-all | bytes 2621440 | tf_op jit(solution)/shard_map/all_to_all | solution.py:165
  206.4 6.4 pack.11
  212.8 14.5 %all-to-all-done.19.refs_1_ = f32[8,2,64,384]{3,2,1,0:T(8,128)S(1)} async-done(((f32[8,2,64,384]{3,2,1,0:T(8,128)}), f32[8,2,64,384]{3,2,1,0:T(8,128)S(1)}, u32[]{:S(2)}, u32[]{:S(2)}) %all-to-all-start.19) | async-done | bytes 1572896 | tf_op jit(solution)/shard_map/all_to_all | solution.py:162
  227.3 25.2 %all_to_all.127.refs_2_ = f32[8,1,64,768]{3,2,1,0:T(8,128)} all-to-all(f32[8,1,64,768]{3,2,1,0:T(8,128)} %bitcast.32), channel_id=1, replica_groups=mesh['ta'=4,'sa'=8] {'sa'}, dimensions={0} | all-to-all | bytes 3145728 | tf_op jit(solution)/shard_map/all_to_all | solution.py:167
  256.1 6.5 pack.10
  262.6 14.4 %all-to-all-done.9.refs_0_ = f32[8,1,64,768]{3,2,1,0:T(8,128)S(1)} async-done(((f32[8,1,64,768]{3,2,1,0:T(8,128)}), f32[8,1,64,768]{3,2,1,0:T(8,128)S(1)}, u32[]{:S(2)}, u32[]{:S(2)}) %all-to-all-start.9) | async-done | bytes 1572896 | tf_op jit(solution)/shard_map/all_to_all | solution.py:165
  277.1 25.5 %all_to_all.128.refs_0_ = f32[8,1,64,768]{3,2,1,0:T(8,128)} all-to-all(f32[8,1,64,768]{3,2,1,0:T(8,128)} %bitcast.33), channel_id=1, replica_groups=mesh['ta'=4,'sa'=8] {'sa'}, dimensions={0} | all-to-all | bytes 3145728 | tf_op jit(solution)/shard_map/all_to_all | solution.py:165
  302.5 24.2 %all_to_all.129.refs_2_ = f32[8,1,64,768]{3,2,1,0:T(8,128)} all-to-all(f32[8,1,64,768]{3,2,1,0:T(8,128)S(1)} %bitcast.31), channel_id=1, replica_groups=mesh['ta'=4,'sa'=8] {'sa'}, dimensions={0} | all-to-all | bytes 3145728 | tf_op jit(solution)/shard_map/all_to_all | solution.py:167
  326.8 29.9 %all_to_all.130.refs_1_ = f32[8,2,64,512]{3,2,1,0:T(8,128)} all-to-all(f32[8,2,64,512]{3,2,1,0:T(8,128)S(1)} %bitcast.27), channel_id=1, replica_groups=mesh['ta'=4,'sa'=8] {'sa'}, dimensions={0} | all-to-all | bytes 4194304 | tf_op jit(solution)/shard_map/all_to_all | solution.py:162
  356.6 29.7 %all_to_all.131.refs_1_ = f32[8,2,64,512]{3,2,1,0:T(8,128)} all-to-all(f32[8,2,64,512]{3,2,1,0:T(8,128)S(1)} %bitcast.28), channel_id=1, replica_groups=mesh['ta'=4,'sa'=8] {'sa'}, dimensions={0} | all-to-all | bytes 4194304 | tf_op jit(solution)/shard_map/all_to_all | solution.py:162
  394.8 5.6 collective-permute-start.28
  401.7 5.5 collective-permute-start.25
  411.2 4.4 collective-permute-start.21
  415.6 6.5 all-to-all-done.13.refs_1_
  427.3 17.9 %collective-permute-done.25.refs_4_ = f32[8,1,64,384]{3,2,1,0:T(8,128)} collective-permute-done((f32[8,1,64,384]{3,2,1,0:T(8,128)}, f32[8,1,64,384]{3,2,1,0:T(8,128)}, u32[]{:S(2)}, u32[]{:S(2)}) %collective-permute-start.25) | collective-permute-done | bytes 786464 | tf_op jit(solution)/shard_map/ppermute | solution.py:168
  445.2 4.5 collective-permute-start.17
  451.0 4.6 collective-permute-start.5
  456.9 10.8 %collective-permute-done.21.refs_4_ = f32[8,1,64,512]{3,2,1,0:T(8,128)} collective-permute-done((f32[8,1,64,512]{3,2,1,0:T(8,128)}, f32[8,1,64,512]{3,2,1,0:T(8,128)}, u32[]{:S(2)}, u32[]{:S(2)}) %collective-permute-start.21) | collective-permute-done | bytes 1048608 | tf_op jit(solution)/shard_map/ppermute | solution.py:168
  468.9 8.8 collective-permute-done.22.refs_5_
  477.8 4.5 collective-permute-start.24
  482.3 35.9 %collective-permute-done.5.refs_4_ = f32[8,1,64,512]{3,2,1,0:T(8,128)S(1)} collective-permute-done((f32[8,1,64,512]{3,2,1,0:T(8,128)}, f32[8,1,64,512]{3,2,1,0:T(8,128)S(1)}, u32[]{:S(2)}, u32[]{:S(2)}) %collective-permute-start.5) | collective-permute-done | bytes 1048608 | tf_op jit(solution)/shard_map/ppermute | solution.py:168
  519.5 6.1 collective-permute-start.13
  530.8 4.5 all-to-all-start.7
  535.2 16.7 %collective-permute-done.24.refs_3_ = f32[8,2,64,384]{3,2,1,0:T(8,128)} collective-permute-done((f32[8,2,64,384]{3,2,1,0:T(8,128)}, f32[8,2,64,384]{3,2,1,0:T(8,128)}, u32[]{:S(2)}, u32[]{:S(2)}) %collective-permute-start.24) | collective-permute-done | bytes 1572896 | tf_op jit(solution)/shard_map/ppermute | solution.py:163
  551.9 4.5 collective-permute-start.9
  556.4 5.8 collective-permute-done.27.refs_6_
  565.7 19.9 %collective-permute-done.13.refs_4_ = f32[8,1,64,768]{3,2,1,0:T(8,128)} collective-permute-done((f32[8,1,64,768]{3,2,1,0:T(8,128)}, f32[8,1,64,768]{3,2,1,0:T(8,128)}, u32[]{:S(2)}, u32[]{:S(2)}) %collective-permute-start.13) | collective-permute-done | bytes 1572896 | tf_op jit(solution)/shard_map/ppermute | solution.py:168
  585.6 5.9 collective-permute-start.16
  591.6 4.3 collective-permute-done.14.refs_5_
  597.2 32.4 %collective-permute-done.10.refs_5_ = f32[8,1,64,768]{3,2,1,0:T(8,128)} collective-permute-done((f32[8,1,64,768]{3,2,1,0:T(8,128)}, f32[8,1,64,768]{3,2,1,0:T(8,128)}, u32[]{:S(2)}, u32[]{:S(2)}) %collective-permute-start.10) | collective-permute-done | bytes 1572896 | tf_op jit(solution)/shard_map/ppermute | solution.py:166
  629.6 4.7 collective-permute-start.4
  635.6 28.7 %collective-permute-done.20.refs_3_ = f32[8,2,64,512]{3,2,1,0:T(8,128)S(1)} collective-permute-done((f32[8,2,64,512]{3,2,1,0:T(8,128)}, f32[8,2,64,512]{3,2,1,0:T(8,128)S(1)}, u32[]{:S(2)}, u32[]{:S(2)}) %collective-permute-start.20) | collective-permute-done | bytes 2097184 | tf_op jit(solution)/shard_map/ppermute | solution.py:163
  664.3 5.9 collective-permute-start.12
  670.2 4.2 collective-permute-done.23.refs_6_
  677.0 88.3 %collective-permute-done.4.refs_3_ = f32[8,2,64,512]{3,2,1,0:T(8,128)} collective-permute-done((f32[8,2,64,512]{3,2,1,0:T(8,128)}, f32[8,2,64,512]{3,2,1,0:T(8,128)}, u32[]{:S(2)}, u32[]{:S(2)}) %collective-permute-start.4) | collective-permute-done | bytes 2097184 | tf_op jit(solution)/shard_map/ppermute | solution.py:163
  766.7 6.8 collective-permute-start.8
  776.4 4.2 all-to-all-start.1
  782.0 14.1 %all-to-all-done.1.refs_1_ = f32[8,2,64,256]{3,2,1,0:T(8,128)} async-done(((f32[8,2,64,256]{3,2,1,0:T(8,128)}), f32[8,2,64,256]{3,2,1,0:T(8,128)}, u32[]{:S(2)}, u32[]{:S(2)}) %all-to-all-start.1) | async-done | bytes 1048608 | tf_op jit(solution)/shard_map/all_to_all | solution.py:162
  796.1 4.1 all-to-all-start.2
  800.2 32.5 %collective-permute-done.12.refs_3_ = f32[8,2,64,768]{3,2,1,0:T(8,128)} collective-permute-done((f32[8,2,64,768]{3,2,1,0:T(8,128)S(1)}, f32[8,2,64,768]{3,2,1,0:T(8,128)}, u32[]{:S(2)}, u32[]{:S(2)}) %collective-permute-start.12) | collective-permute-done | bytes 3145760 | tf_op jit(solution)/shard_map/ppermute | solution.py:163
  832.7 5.5 collective-permute-start
  839.5 4.1 all-to-all-start
  843.6 21.9 %collective-permute-done.11.refs_6_ = f32[8,2,64,768]{3,2,1,0:T(8,128)} collective-permute-done((f32[8,2,64,768]{3,2,1,0:T(8,128)}, f32[8,2,64,768]{3,2,1,0:T(8,128)}, u32[]{:S(2)}, u32[]{:S(2)}) %collective-permute-start.11) | collective-permute-done | bytes 3145760 | tf_op jit(solution)/shard_map/ppermute | solution.py:164
  869.0 31.2 %collective-permute-done.8.refs_3_ = f32[8,2,64,768]{3,2,1,0:T(8,128)} collective-permute-done((f32[8,2,64,768]{3,2,1,0:T(8,128)}, f32[8,2,64,768]{3,2,1,0:T(8,128)}, u32[]{:S(2)}, u32[]{:S(2)}) %collective-permute-start.8) | collective-permute-done | bytes 3145760 | tf_op jit(solution)/shard_map/ppermute | solution.py:163
  901.5 4.0 smooth.8.refs_7_
  905.5 6.3 smooth.9.refs_7_
  911.8 7.2 smooth.10.refs_7_
  919.0 9.4 smooth.11.refs_7_
  928.4 10.3 %smooth.12.refs_7_ = f32[8,4,512,512]{3,2,1,0:T(8,128)} custom-call(f32[7]{0:T(128)} %taps_ref.15, f32[8,1,64,768]{3,2,1,0:T(8,128)} %copy-done.2, f32[8,2,64,768]{3,2,1,0:T(8,128)} %copy-done, f32[8,1,64,768]{3,2,1,0:T(8,128)} %all_to_all.127.refs_2_, f32[8,2,64,768]{3,2,1,0:T(8,128)} %collective-permute-done.12.refs_3_, ...), custom_call_target="tpu_custom_call", output_to_operand_aliasing={{}: (8, {})} | custom-call | flops 22020096 | bytes 22020096 | tf_op jit(solution)/shard_map/smooth/pallas_call | solution.py:126
  938.7 10.3 %smooth.13.refs_7_ = f32[8,4,512,512]{3,2,1,0:T(8,128)} custom-call(f32[7]{0:T(128)} %taps_ref.15, f32[8,1,64,768]{3,2,1,0:T(8,128)} %all_to_all.128.refs_0_, f32[8,2,64,768]{3,2,1,0:T(8,128)} %all-to-all-done.7.refs_1_, f32[8,1,64,768]{3,2,1,0:T(8,128)} %all_to_all.129.refs_2_, ...), custom_call_target="tpu_custom_call", output_to_operand_aliasing={{}: (8, {})} | custom-call | flops 22020096 | bytes 22020096 | tf_op jit(solution)/shard_map/smooth/pallas_call | solution.py:126
  949.0 7.2 smooth.14.refs_7_
  (108 shorter events, 83.3 us)
Async XLA Ops:
  17.9 372.1 %copy-start.7 = (f32[8,1,64,256]{3,2,1,0:T(8,128)}, f32[8,1,64,256]{3,2,1,0:T(8,128)S(1)}, u32[]{:S(2)}) copy-start(f32[8,1,64,256]{3,2,1,0:T(8,128)S(1)} %all_to_all.120.refs_2_) | copy-start | bytes 1572868
  17.9 13.1 %all-to-all-start.21 = ((f32[8,1,64,256]{3,2,1,0:T(8,128)}), f32[8,1,64,256]{3,2,1,0:T(8,128)S(1)}, u32[]{:S(2)}, u32[]{:S(2)}) async-start(f32[8,1,64,256]{3,2,1,0:T(8,128)} %bitcast.43), calls=%async_computation.21 | async-start | bytes 1048576 | tf_op jit(solution)/shard_map/all_to_all | solution.py:165
  25.8 21.9 %copy-start.23 = (f32[8,1,1,64,384]{4,3,2,1,0:T(8,128)S(1)}, f32[8,1,1,64,384]{4,3,2,1,0:T(8,128)}, u32[]{:S(2)}) copy-start(f32[8,1,1,64,384]{4,3,2,1,0:T(8,128)} %get-tuple-element.47) | copy-start | bytes 2359300
  31.0 32.3 %copy-start.8 = (f32[8,1,64,256]{3,2,1,0:T(8,128)}, f32[8,1,64,256]{3,2,1,0:T(8,128)S(1)}, u32[]{:S(2)}) copy-start(f32[8,1,64,256]{3,2,1,0:T(8,128)S(1)} %all-to-all-done.21.refs_0_) | copy-start | bytes 1572868
  63.4 18.9 %all-to-all-start.22 = ((f32[8,2,64,256]{3,2,1,0:T(8,128)}), f32[8,2,64,256]{3,2,1,0:T(8,128)S(1)}, u32[]{:S(2)}, u32[]{:S(2)}) async-start(f32[8,2,64,256]{3,2,1,0:T(8,128)} %bitcast.22), calls=%async_computation.22 | async-start | bytes 2097152 | tf_op jit(solution)/shard_map/all_to_all | solution.py:162
  82.2 19.5 %copy-start.6 = (f32[8,2,64,256]{3,2,1,0:T(8,128)}, f32[8,2,64,256]{3,2,1,0:T(8,128)S(1)}, u32[]{:S(2)}) copy-start(f32[8,2,64,256]{3,2,1,0:T(8,128)S(1)} %all-to-all-done.22.refs_1_) | copy-start | bytes 3145732
  101.8 18.9 %all-to-all-start.15 = ((f32[8,1,64,512]{3,2,1,0:T(8,128)}), f32[8,1,64,512]{3,2,1,0:T(8,128)S(1)}, u32[]{:S(2)}, u32[]{:S(2)}) async-start(f32[8,1,64,512]{3,2,1,0:T(8,128)} %bitcast.15), calls=%async_computation.15 | async-start | bytes 2097152 | tf_op jit(solution)/shard_map/all_to_all | solution.py:165
  120.7 19.6 %copy-start.5 = (f32[8,1,64,512]{3,2,1,0:T(8,128)}, f32[8,1,64,512]{3,2,1,0:T(8,128)S(1)}, u32[]{:S(2)}) copy-start(f32[8,1,64,512]{3,2,1,0:T(8,128)S(1)} %all-to-all-done.15.refs_0_) | copy-start | bytes 3145732
  140.2 18.9 %all-to-all-start.3 = ((f32[8,1,64,512]{3,2,1,0:T(8,128)}), f32[8,1,64,512]{3,2,1,0:T(8,128)S(1)}, u32[]{:S(2)}, u32[]{:S(2)}) async-start(f32[8,1,64,512]{3,2,1,0:T(8,128)} %bitcast.3), calls=%async_computation.3 | async-start | bytes 2097152 | tf_op jit(solution)/shard_map/all_to_all | solution.py:165
  150.4 31.2 %copy-start.16 = (f32[8,1,1,64,640]{4,3,2,1,0:T(8,128)S(1)}, f32[8,1,1,64,640]{4,3,2,1,0:T(8,128)}, u32[]{:S(2)}) copy-start(f32[8,1,1,64,640]{4,3,2,1,0:T(8,128)} %get-tuple-element.41) | copy-start | bytes 3932164
  159.1 43.7 %copy-start.4 = (f32[8,1,64,512]{3,2,1,0:T(8,128)}, f32[8,1,64,512]{3,2,1,0:T(8,128)S(1)}, u32[]{:S(2)}) copy-start(f32[8,1,64,512]{3,2,1,0:T(8,128)S(1)} %all-to-all-done.3.refs_0_) | copy-start | bytes 3145732
  202.8 24.5 %all-to-all-start.19 = ((f32[8,2,64,384]{3,2,1,0:T(8,128)}), f32[8,2,64,384]{3,2,1,0:T(8,128)S(1)}, u32[]{:S(2)}, u32[]{:S(2)}) async-start(f32[8,2,64,384]{3,2,1,0:T(8,128)} %bitcast.29), calls=%async_computation.19 | async-start | bytes 3145728 | tf_op jit(solution)/shard_map/all_to_all | solution.py:162
  227.3 25.2 %copy-start.3 = (f32[8,2,64,384]{3,2,1,0:T(8,128)}, f32[8,2,64,384]{3,2,1,0:T(8,128)S(1)}, u32[]{:S(2)}) copy-start(f32[8,2,64,384]{3,2,1,0:T(8,128)S(1)} %all-to-all-done.19.refs_1_) | copy-start | bytes 4718596
  252.5 24.5 %all-to-all-start.9 = ((f32[8,1,64,768]{3,2,1,0:T(8,128)}), f32[8,1,64,768]{3,2,1,0:T(8,128)S(1)}, u32[]{:S(2)}, u32[]{:S(2)}) async-start(f32[8,1,64,768]{3,2,1,0:T(8,128)} %bitcast.30), calls=%async_computation.9 | async-start | bytes 3145728 | tf_op jit(solution)/shard_map/all_to_all | solution.py:165
  277.0 49.7 %copy-start.2 = (f32[8,1,64,768]{3,2,1,0:T(8,128)}, f32[8,1,64,768]{3,2,1,0:T(8,128)S(1)}, u32[]{:S(2)}) copy-start(f32[8,1,64,768]{3,2,1,0:T(8,128)S(1)} %all-to-all-done.9.refs_0_) | copy-start | bytes 4718596
  277.1 25.5 %copy-start.14 = (f32[8,1,1,64,768]{4,3,2,1,0:T(8,128)S(1)}, f32[8,1,1,64,768]{4,3,2,1,0:T(8,128)}, u32[]{:S(2)}) copy-start(f32[8,1,1,64,768]{4,3,2,1,0:T(8,128)} %get-tuple-element.37) | copy-start | bytes 4718596
  302.5 24.2 %copy-start.12 = (f32[8,1,2,64,512]{4,3,2,1,0:T(8,128)S(1)}, f32[8,1,2,64,512]{4,3,2,1,0:T(8,128)}, u32[]{:S(2)}) copy-start(f32[8,1,2,64,512]{4,3,2,1,0:T(8,128)} %get-tuple-element.45) | copy-start | bytes 6291460
  326.7 29.9 %copy-start.13 = (f32[8,1,2,64,512]{4,3,2,1,0:T(8,128)S(1)}, f32[8,1,2,64,512]{4,3,2,1,0:T(8,128)}, u32[]{:S(2)}) copy-start(f32[8,1,2,64,512]{4,3,2,1,0:T(8,128)} %get-tuple-element.33) | copy-start | bytes 6291460
  386.3 35.8 %all-to-all-start.13 = ((f32[8,2,64,640]{3,2,1,0:T(8,128)}), f32[8,2,64,640]{3,2,1,0:T(8,128)S(1)}, u32[]{:S(2)}, u32[]{:S(2)}) async-start(f32[8,2,64,640]{3,2,1,0:T(8,128)} %bitcast.26), calls=%async_computation.13 | async-start | bytes 5242880 | tf_op jit(solution)/shard_map/all_to_all | solution.py:162
  390.0 17.2 %collective-permute-start.29 = (f32[8,1,64,256]{3,2,1,0:T(8,128)S(1)}, f32[8,1,64,256]{3,2,1,0:T(8,128)S(1)}, u32[]{:S(2)}, u32[]{:S(2)}) collective-permute-start(f32[8,1,64,256]{3,2,1,0:T(8,128)S(1)} %all_to_all.120.refs_2_), channel_id=1, source_target_pairs={{0,8},{8,16},{16,24},{1,9},{9,17},{17,25},{2,10},{10,18},{18,26},{... | collective-permute-start | bytes 1572872 | tf_op jit(solution)/shard_map/ppermute | solution.py:168
  393.5 16.9 %collective-permute-start.30 = (f32[8,1,64,256]{3,2,1,0:T(8,128)}, f32[8,1,64,256]{3,2,1,0:T(8,128)S(1)}, u32[]{:S(2)}, u32[]{:S(2)}) collective-permute-start(f32[8,1,64,256]{3,2,1,0:T(8,128)} %copy-done.8), channel_id=1, source_target_pairs={{8,0},{16,8},{24,16},{9,1},{17,9},{25,17},{10,2},{18,10},{26,18},{... | collective-permute-start | bytes 1572872 | tf_op jit(solution)/shard_map/ppermute | solution.py:166
  394.8 56.2 %collective-permute-start.28 = (f32[8,2,64,256]{3,2,1,0:T(8,128)}, f32[8,2,64,256]{3,2,1,0:T(8,128)}, u32[]{:S(2)}, u32[]{:S(2)}) collective-permute-start(f32[8,2,64,256]{3,2,1,0:T(8,128)} %copy-done.6), channel_id=1, source_target_pairs={{0,8},{8,16},{16,24},{1,9},{9,17},{17,25},{2,10},{10,18},{18,26},{... | collective-permute-start | bytes 3145736 | tf_op jit(solution)/shard_map/ppermute | solution.py:163
  400.4 55.2 %collective-permute-start.31 = (f32[8,2,64,256]{3,2,1,0:T(8,128)}, f32[8,2,64,256]{3,2,1,0:T(8,128)}, u32[]{:S(2)}, u32[]{:S(2)}) collective-permute-start(f32[8,2,64,256]{3,2,1,0:T(8,128)} %copy-done.6), channel_id=1, source_target_pairs={{8,0},{16,8},{24,16},{9,1},{17,9},{25,17},{10,2},{18,10},{26,18},{... | collective-permute-start | bytes 3145736 | tf_op jit(solution)/shard_map/ppermute | solution.py:164
  401.7 43.5 %collective-permute-start.25 = (f32[8,1,64,384]{3,2,1,0:T(8,128)}, f32[8,1,64,384]{3,2,1,0:T(8,128)}, u32[]{:S(2)}, u32[]{:S(2)}) collective-permute-start(f32[8,1,64,384]{3,2,1,0:T(8,128)} %all_to_all.121.refs_2_), channel_id=1, source_target_pairs={{0,8},{8,16},{16,24},{1,9},{9,17},{17,25},{2,10},{10,18},{18,26},{... | collective-permute-start | bytes 2359304 | tf_op jit(solution)/shard_map/ppermute | solution.py:168
  407.1 3.2 copy-start.24
  407.2 42.5 %collective-permute-start.26 = (f32[8,1,64,384]{3,2,1,0:T(8,128)}, f32[8,1,64,384]{3,2,1,0:T(8,128)}, u32[]{:S(2)}, u32[]{:S(2)}) collective-permute-start(f32[8,1,64,384]{3,2,1,0:T(8,128)} %all_to_all.122.refs_0_), channel_id=1, source_target_pairs={{8,0},{16,8},{24,16},{9,1},{17,9},{25,17},{10,2},{18,10},{26,18},{... | collective-permute-start | bytes 2359304 | tf_op jit(solution)/shard_map/ppermute | solution.py:166
  411.2 56.5 %collective-permute-start.21 = (f32[8,1,64,512]{3,2,1,0:T(8,128)}, f32[8,1,64,512]{3,2,1,0:T(8,128)}, u32[]{:S(2)}, u32[]{:S(2)}) collective-permute-start(f32[8,1,64,512]{3,2,1,0:T(8,128)} %all_to_all.123.refs_2_), channel_id=1, source_target_pairs={{0,8},{8,16},{16,24},{1,9},{9,17},{17,25},{2,10},{10,18},{18,26},{... | collective-permute-start | bytes 3145736 | tf_op jit(solution)/shard_map/ppermute | solution.py:168
  423.6 107.1 %all-to-all-start.10 = ((f32[8,2,64,768]{3,2,1,0:T(8,128)}), f32[8,2,64,768]{3,2,1,0:T(8,128)S(1)}, u32[]{:S(2)}, u32[]{:S(2)}) async-start(f32[8,2,64,768]{3,2,1,0:T(8,128)} %bitcast.25), calls=%async_computation.10 | async-start | bytes 6291456 | tf_op jit(solution)/shard_map/all_to_all | solution.py:162
  445.2 80.4 %collective-permute-start.17 = (f32[8,1,64,640]{3,2,1,0:T(8,128)}, f32[8,1,64,640]{3,2,1,0:T(8,128)S(1)}, u32[]{:S(2)}, u32[]{:S(2)}) collective-permute-start(f32[8,1,64,640]{3,2,1,0:T(8,128)} %all_to_all.125.refs_2_), channel_id=1, source_target_pairs={{0,8},{8,16},{16,24},{1,9},{9,17},{17,25},{2,10},{10,18},{18,26},{... | collective-permute-start | bytes 3932168 | tf_op jit(solution)/shard_map/ppermute | solution.py:168
  449.7 28.1 %collective-permute-start.22 = (f32[8,1,64,512]{3,2,1,0:T(8,128)}, f32[8,1,64,512]{3,2,1,0:T(8,128)S(1)}, u32[]{:S(2)}, u32[]{:S(2)}) collective-permute-start(f32[8,1,64,512]{3,2,1,0:T(8,128)} %copy-done.5), channel_id=1, source_target_pairs={{8,0},{16,8},{24,16},{9,1},{17,9},{25,17},{10,2},{18,10},{26,18},{... | collective-permute-start | bytes 3145736 | tf_op jit(solution)/shard_map/ppermute | solution.py:166
  451.0 67.2 %collective-permute-start.5 = (f32[8,1,64,512]{3,2,1,0:T(8,128)}, f32[8,1,64,512]{3,2,1,0:T(8,128)S(1)}, u32[]{:S(2)}, u32[]{:S(2)}) collective-permute-start(f32[8,1,64,512]{3,2,1,0:T(8,128)} %all_to_all.124.refs_2_), channel_id=1, source_target_pairs={{0,8},{8,16},{16,24},{1,9},{9,17},{17,25},{2,10},{10,18},{18,26},{... | collective-permute-start | bytes 3145736 | tf_op jit(solution)/shard_map/ppermute | solution.py:168
  455.6 63.9 %collective-permute-start.6 = (f32[8,1,64,512]{3,2,1,0:T(8,128)}, f32[8,1,64,512]{3,2,1,0:T(8,128)S(1)}, u32[]{:S(2)}, u32[]{:S(2)}) collective-permute-start(f32[8,1,64,512]{3,2,1,0:T(8,128)} %copy-done.4), channel_id=1, source_target_pairs={{8,0},{16,8},{24,16},{9,1},{17,9},{25,17},{10,2},{18,10},{26,18},{... | collective-permute-start | bytes 3145736 | tf_op jit(solution)/shard_map/ppermute | solution.py:166
  467.7 60.7 %collective-permute-start.18 = (f32[8,1,64,640]{3,2,1,0:T(8,128)}, f32[8,1,64,640]{3,2,1,0:T(8,128)S(1)}, u32[]{:S(2)}, u32[]{:S(2)}) collective-permute-start(f32[8,1,64,640]{3,2,1,0:T(8,128)} %all_to_all.126.refs_0_), channel_id=1, source_target_pairs={{8,0},{16,8},{24,16},{9,1},{17,9},{25,17},{10,2},{18,10},{26,18},{... | collective-permute-start | bytes 3932168 | tf_op jit(solution)/shard_map/ppermute | solution.py:166
  477.8 50.6 %copy-start.21 = (f32[8,1,64,512]{3,2,1,0:T(8,128)}, f32[8,1,64,512]{3,2,1,0:T(8,128)S(1)}, u32[]{:S(2)}) copy-start(f32[8,1,64,512]{3,2,1,0:T(8,128)S(1)} %collective-permute-done.22.refs_5_) | copy-start | bytes 3145732
  477.8 74.1 %collective-permute-start.24 = (f32[8,2,64,384]{3,2,1,0:T(8,128)}, f32[8,2,64,384]{3,2,1,0:T(8,128)}, u32[]{:S(2)}, u32[]{:S(2)}) collective-permute-start(f32[8,2,64,384]{3,2,1,0:T(8,128)} %copy-done.3), channel_id=1, source_target_pairs={{0,8},{8,16},{16,24},{1,9},{9,17},{17,25},{2,10},{10,18},{18,26},{... | collective-permute-start | bytes 4718600 | tf_op jit(solution)/shard_map/ppermute | solution.py:163
  518.2 10.1 %copy-start.19 = (f32[8,1,64,512]{3,2,1,0:T(8,128)}, f32[8,1,64,512]{3,2,1,0:T(8,128)S(1)}, u32[]{:S(2)}) copy-start(f32[8,1,64,512]{3,2,1,0:T(8,128)S(1)} %collective-permute-done.5.refs_4_) | copy-start | bytes 3145732
  518.2 43.9 %collective-permute-start.27 = (f32[8,2,64,384]{3,2,1,0:T(8,128)}, f32[8,2,64,384]{3,2,1,0:T(8,128)}, u32[]{:S(2)}, u32[]{:S(2)}) collective-permute-start(f32[8,2,64,384]{3,2,1,0:T(8,128)} %copy-done.3), channel_id=1, source_target_pairs={{8,0},{16,8},{24,16},{9,1},{17,9},{25,17},{10,2},{18,10},{26,18},{... | collective-permute-start | bytes 4718600 | tf_op jit(solution)/shard_map/ppermute | solution.py:164
  519.5 8.8 copy-start.20
  519.5 66.1 %collective-permute-start.13 = (f32[8,1,64,768]{3,2,1,0:T(8,128)}, f32[8,1,64,768]{3,2,1,0:T(8,128)}, u32[]{:S(2)}, u32[]{:S(2)}) collective-permute-start(f32[8,1,64,768]{3,2,1,0:T(8,128)} %all_to_all.127.refs_2_), channel_id=1, source_target_pairs={{0,8},{8,16},{16,24},{1,9},{9,17},{17,25},{2,10},{10,18},{18,26},{... | collective-permute-start | bytes 4718600 | tf_op jit(solution)/shard_map/ppermute | solution.py:168
  525.6 70.3 %collective-permute-start.14 = (f32[8,1,64,768]{3,2,1,0:T(8,128)}, f32[8,1,64,768]{3,2,1,0:T(8,128)}, u32[]{:S(2)}, u32[]{:S(2)}) collective-permute-start(f32[8,1,64,768]{3,2,1,0:T(8,128)} %copy-done.2), channel_id=1, source_target_pairs={{8,0},{16,8},{24,16},{9,1},{17,9},{25,17},{10,2},{18,10},{26,18},{... | collective-permute-start | bytes 4718600 | tf_op jit(solution)/shard_map/ppermute | solution.py:166
  529.4 100.1 %collective-permute-start.10 = (f32[8,1,64,768]{3,2,1,0:T(8,128)}, f32[8,1,64,768]{3,2,1,0:T(8,128)}, u32[]{:S(2)}, u32[]{:S(2)}) collective-permute-start(f32[8,1,64,768]{3,2,1,0:T(8,128)} %all_to_all.128.refs_0_), channel_id=1, source_target_pairs={{8,0},{16,8},{24,16},{9,1},{17,9},{25,17},{10,2},{18,10},{26,18},{... | collective-permute-start | bytes 4718600 | tf_op jit(solution)/shard_map/ppermute | solution.py:166
  530.7 143.7 %copy-start = (f32[8,2,64,768]{3,2,1,0:T(8,128)}, f32[8,2,64,768]{3,2,1,0:T(8,128)S(1)}, u32[]{:S(2)}) copy-start(f32[8,2,64,768]{3,2,1,0:T(8,128)S(1)} %all-to-all-done.10.refs_1_) | copy-start | bytes 9437188
  530.8 146.3 %all-to-all-start.7 = ((f32[8,2,64,768]{3,2,1,0:T(8,128)}), f32[8,2,64,768]{3,2,1,0:T(8,128)}, u32[]{:S(2)}, u32[]{:S(2)}) async-start(f32[8,2,64,768]{3,2,1,0:T(8,128)} %bitcast.24), calls=%async_computation.7 | async-start | bytes 6291456 | tf_op jit(solution)/shard_map/all_to_all | solution.py:162
  551.9 82.4 %collective-permute-start.9 = (f32[8,1,64,768]{3,2,1,0:T(8,128)}, f32[8,1,64,768]{3,2,1,0:T(8,128)S(1)}, u32[]{:S(2)}, u32[]{:S(2)}) collective-permute-start(f32[8,1,64,768]{3,2,1,0:T(8,128)} %all_to_all.129.refs_2_), channel_id=1, source_target_pairs={{0,8},{8,16},{16,24},{1,9},{9,17},{17,25},{2,10},{10,18},{18,26},{... | collective-permute-start | bytes 4718600 | tf_op jit(solution)/shard_map/ppermute | solution.py:168
  562.2 102.1 %collective-permute-start.20 = (f32[8,2,64,512]{3,2,1,0:T(8,128)}, f32[8,2,64,512]{3,2,1,0:T(8,128)S(1)}, u32[]{:S(2)}, u32[]{:S(2)}) collective-permute-start(f32[8,2,64,512]{3,2,1,0:T(8,128)} %all_to_all.130.refs_1_), channel_id=1, source_target_pairs={{0,8},{8,16},{16,24},{1,9},{9,17},{17,25},{2,10},{10,18},{18,26},{... | collective-permute-start | bytes 6291464 | tf_op jit(solution)/shard_map/ppermute | solution.py:163
  585.6 181.1 %collective-permute-start.16 = (f32[8,2,64,640]{3,2,1,0:T(8,128)}, f32[8,2,64,640]{3,2,1,0:T(8,128)}, u32[]{:S(2)}, u32[]{:S(2)}) collective-permute-start(f32[8,2,64,640]{3,2,1,0:T(8,128)} %copy-done.1), channel_id=1, source_target_pairs={{0,8},{8,16},{16,24},{1,9},{9,17},{17,25},{2,10},{10,18},{18,26},{... | collective-permute-start | bytes 7864328 | tf_op jit(solution)/shard_map/ppermute | solution.py:163
  595.9 78.5 %collective-permute-start.23 = (f32[8,2,64,512]{3,2,1,0:T(8,128)}, f32[8,2,64,512]{3,2,1,0:T(8,128)S(1)}, u32[]{:S(2)}, u32[]{:S(2)}) collective-permute-start(f32[8,2,64,512]{3,2,1,0:T(8,128)} %all_to_all.130.refs_1_), channel_id=1, source_target_pairs={{8,0},{16,8},{24,16},{9,1},{17,9},{25,17},{10,2},{18,10},{26,18},{... | collective-permute-start | bytes 6291464 | tf_op jit(solution)/shard_map/ppermute | solution.py:164
  629.6 135.8 %collective-permute-start.4 = (f32[8,2,64,512]{3,2,1,0:T(8,128)}, f32[8,2,64,512]{3,2,1,0:T(8,128)}, u32[]{:S(2)}, u32[]{:S(2)}) collective-permute-start(f32[8,2,64,512]{3,2,1,0:T(8,128)} %all_to_all.131.refs_1_), channel_id=1, source_target_pairs={{0,8},{8,16},{16,24},{1,9},{9,17},{17,25},{2,10},{10,18},{18,26},{... | collective-permute-start | bytes 6291464 | tf_op jit(solution)/shard_map/ppermute | solution.py:163
  634.3 40.1 %copy-start.15 = (f32[8,1,64,768]{3,2,1,0:T(8,128)}, f32[8,1,64,768]{3,2,1,0:T(8,128)S(1)}, u32[]{:S(2)}) copy-start(f32[8,1,64,768]{3,2,1,0:T(8,128)S(1)} %collective-permute-done.9.refs_4_) | copy-start | bytes 4718596
  634.3 146.4 %collective-permute-start.19 = (f32[8,2,64,640]{3,2,1,0:T(8,128)}, f32[8,2,64,640]{3,2,1,0:T(8,128)}, u32[]{:S(2)}, u32[]{:S(2)}) collective-permute-start(f32[8,2,64,640]{3,2,1,0:T(8,128)} %copy-done.1), channel_id=1, source_target_pairs={{8,0},{16,8},{24,16},{9,1},{17,9},{25,17},{10,2},{18,10},{26,18},{... | collective-permute-start | bytes 7864328 | tf_op jit(solution)/shard_map/ppermute | solution.py:164
  664.3 5.9 copy-start.10
  664.3 168.4 %collective-permute-start.12 = (f32[8,2,64,768]{3,2,1,0:T(8,128)S(1)}, f32[8,2,64,768]{3,2,1,0:T(8,128)}, u32[]{:S(2)}, u32[]{:S(2)}) collective-permute-start(f32[8,2,64,768]{3,2,1,0:T(8,128)S(1)} %all-to-all-done.10.refs_1_), channel_id=1, source_target_pairs={{0,8},{8,16},{16,24},{1,9},{9,17},{17,25},{2,10},{10,18},{18,26},{... | collective-permute-start | bytes 9437192 | tf_op jit(solution)/shard_map/ppermute | solution.py:163
  675.7 162.5 %collective-permute-start.15 = (f32[8,2,64,768]{3,2,1,0:T(8,128)S(1)}, f32[8,2,64,768]{3,2,1,0:T(8,128)}, u32[]{:S(2)}, u32[]{:S(2)}) collective-permute-start(f32[8,2,64,768]{3,2,1,0:T(8,128)S(1)} %all-to-all-done.10.refs_1_), channel_id=1, source_target_pairs={{8,0},{16,8},{24,16},{9,1},{17,9},{25,17},{10,2},{18,10},{26,18},{... | collective-permute-start | bytes 9437192 | tf_op jit(solution)/shard_map/ppermute | solution.py:164
  765.4 100.1 %collective-permute-start.11 = (f32[8,2,64,768]{3,2,1,0:T(8,128)}, f32[8,2,64,768]{3,2,1,0:T(8,128)}, u32[]{:S(2)}, u32[]{:S(2)}) collective-permute-start(f32[8,2,64,768]{3,2,1,0:T(8,128)} %all-to-all-done.7.refs_1_), channel_id=1, source_target_pairs={{8,0},{16,8},{24,16},{9,1},{17,9},{25,17},{10,2},{18,10},{26,18},{... | collective-permute-start | bytes 9437192 | tf_op jit(solution)/shard_map/ppermute | solution.py:164
  766.7 133.5 %collective-permute-start.8 = (f32[8,2,64,768]{3,2,1,0:T(8,128)}, f32[8,2,64,768]{3,2,1,0:T(8,128)}, u32[]{:S(2)}, u32[]{:S(2)}) collective-permute-start(f32[8,2,64,768]{3,2,1,0:T(8,128)} %all-to-all-done.7.refs_1_), channel_id=1, source_target_pairs={{0,8},{8,16},{16,24},{1,9},{9,17},{17,25},{2,10},{10,18},{18,26},{... | collective-permute-start | bytes 9437192 | tf_op jit(solution)/shard_map/ppermute | solution.py:163
  776.4 19.6 %all-to-all-start.1 = ((f32[8,2,64,256]{3,2,1,0:T(8,128)}), f32[8,2,64,256]{3,2,1,0:T(8,128)}, u32[]{:S(2)}, u32[]{:S(2)}) async-start(f32[8,2,64,256]{3,2,1,0:T(8,128)} %bitcast.36), calls=%async_computation.1 | async-start | bytes 2097152 | tf_op jit(solution)/shard_map/all_to_all | solution.py:162
  780.7 168.3 %collective-permute-start.7 = (f32[8,2,64,512]{3,2,1,0:T(8,128)}, f32[8,2,64,512]{3,2,1,0:T(8,128)}, u32[]{:S(2)}, u32[]{:S(2)}) collective-permute-start(f32[8,2,64,512]{3,2,1,0:T(8,128)} %all_to_all.131.refs_1_), channel_id=1, source_target_pairs={{8,0},{16,8},{24,16},{9,1},{17,9},{25,17},{10,2},{18,10},{26,18},{... | collective-permute-start | bytes 6291464 | tf_op jit(solution)/shard_map/ppermute | solution.py:164
  796.1 43.4 %all-to-all-start.2 = ((f32[8,1,64,256]{3,2,1,0:T(8,128)}), f32[8,1,64,256]{3,2,1,0:T(8,128)}, u32[]{:S(2)}, u32[]{:S(2)}) async-start(f32[8,1,64,256]{3,2,1,0:T(8,128)} %bitcast.42), calls=%async_computation.2 | async-start | bytes 1048576 | tf_op jit(solution)/shard_map/all_to_all | solution.py:167
  832.7 123.6 %collective-permute-start = (f32[8,2,64,256]{3,2,1,0:T(8,128)}, f32[8,2,64,256]{3,2,1,0:T(8,128)}, u32[]{:S(2)}, u32[]{:S(2)}) collective-permute-start(f32[8,2,64,256]{3,2,1,0:T(8,128)} %all-to-all-done.1.refs_1_), channel_id=1, source_target_pairs={{0,8},{8,16},{16,24},{1,9},{9,17},{17,25},{2,10},{10,18},{18,26},{... | collective-permute-start | bytes 3145736 | tf_op jit(solution)/shard_map/ppermute | solution.py:163
  838.2 118.1 %collective-permute-start.3 = (f32[8,2,64,256]{3,2,1,0:T(8,128)}, f32[8,2,64,256]{3,2,1,0:T(8,128)S(1)}, u32[]{:S(2)}, u32[]{:S(2)}) collective-permute-start(f32[8,2,64,256]{3,2,1,0:T(8,128)} %all-to-all-done.1.refs_1_), channel_id=1, source_target_pairs={{8,0},{16,8},{24,16},{9,1},{17,9},{25,17},{10,2},{18,10},{26,18},{... | collective-permute-start | bytes 3145736 | tf_op jit(solution)/shard_map/ppermute | solution.py:164
  839.5 29.4 %all-to-all-start = ((f32[8,1,64,256]{3,2,1,0:T(8,128)}), f32[8,1,64,256]{3,2,1,0:T(8,128)S(1)}, u32[]{:S(2)}, u32[]{:S(2)}) async-start(f32[8,1,64,256]{3,2,1,0:T(8,128)} %bitcast.41), calls=%async_computation | async-start | bytes 1048576 | tf_op jit(solution)/shard_map/all_to_all | solution.py:165
  865.5 90.7 %collective-permute-start.1 = (f32[8,1,64,256]{3,2,1,0:T(8,128)}, f32[8,1,64,256]{3,2,1,0:T(8,128)S(1)}, u32[]{:S(2)}, u32[]{:S(2)}) collective-permute-start(f32[8,1,64,256]{3,2,1,0:T(8,128)} %all-to-all-done.2.refs_2_), channel_id=1, source_target_pairs={{0,8},{8,16},{16,24},{1,9},{9,17},{17,25},{2,10},{10,18},{18,26},{... | collective-permute-start | bytes 1572872 | tf_op jit(solution)/shard_map/ppermute | solution.py:168
  869.0 36.6 %copy-start.9 = (f32[8,1,64,256]{3,2,1,0:T(8,128)}, f32[8,1,64,256]{3,2,1,0:T(8,128)S(1)}, u32[]{:S(2)}) copy-start(f32[8,1,64,256]{3,2,1,0:T(8,128)S(1)} %all-to-all-done.refs_0_) | copy-start | bytes 1572868
  900.2 56.0 %collective-permute-start.2 = (f32[8,1,64,256]{3,2,1,0:T(8,128)S(1)}, f32[8,1,64,256]{3,2,1,0:T(8,128)S(1)}, u32[]{:S(2)}, u32[]{:S(2)}) collective-permute-start(f32[8,1,64,256]{3,2,1,0:T(8,128)S(1)} %all-to-all-done.refs_0_), channel_id=1, source_target_pairs={{8,0},{16,8},{24,16},{9,1},{17,9},{25,17},{10,2},{18,10},{26,18},{... | collective-permute-start | bytes 1572872 | tf_op jit(solution)/shard_map/ppermute | solution.py:166
  (8 other events, 10.1 us)

commit v2 on v1

--- a/solution.py
+++ b/solution.py
@@ -13,18 +13,136 @@
 REACH = 3
 LANES = 128
 SUBLANES = 8
-SHARES = (2, 3, 4, 5, 6, 6, 4, 2)
+EARLY = (2, 8)
+LATE = (18, 4)
 
 
 def chunk_bounds(width):
     units = width // LANES
-    edges, seen = [0], 0
-    for share in SHARES:
-        seen += share
-        edge = units * seen // sum(SHARES)
-        if edge > edges[-1]:
-            edges.append(edge)
-    return [(a * LANES, b * LANES) for a, b in zip(edges, edges[1:])]
+    shares = EARLY + LATE
+    edges = [units * sum(shares[:i]) // sum(shares) for i in range(len(shares) + 1)]
+    bounds = [(a * LANES, b * LANES) for a, b in zip(edges, edges[1:])]
+    early = [b for b in bounds[: len(EARLY)] if b[0] < b[1]]
+    late = [b for b in bounds[len(EARLY) :] if b[0] < b[1]]
+    return early, late
+
+
+def weighted(taps, field, t):
+    total = taps[0] * field[t]
+    for j in range(1, 2 * REACH + 1):
+        total = total + taps[j] * field[t + j]
+    return total
+
+
+def raw_kernel(frames_ref, up_ref, down_ref):
+    steps = frames_ref.shape[0]
+    for t in range(REACH):
+        up_ref[t] = frames_ref[steps - REACH + t, 0]
+        down_ref[t] = frames_ref[t, 0]
+
+
+def raw_chunk(frames, span, start, width):
+    steps, _, strip, columns = frames.shape
+    groups = columns // span
+    block = math.gcd(math.gcd(start, width), span)
+    side = jax.ShapeDtypeStruct((REACH, strip, groups * width), jnp.float32)
+    per_group = width // block
+    elements = strip * groups * width
+    return pl.pallas_call(
+        raw_kernel,
+        grid=(groups, per_group),
+        out_shape=[side, side],
+        in_specs=[
+            pl.BlockSpec(
+                (steps, 1, strip, block),
+                lambda g, i: (0, 0, 0, g * (span // block) + start // block + i),
+            )
+        ],
+        out_specs=[
+            pl.BlockSpec((REACH, strip, block), lambda g, i: (0, 0, g * per_group + i))
+        ]
+        * 2,
+        cost_estimate=pl.CostEstimate(
+            flops=elements, bytes_accessed=4 * (steps + 2 * REACH) * elements, transcendentals=0
+        ),
+        name="raw",
+    )(frames)
+
+
+def early_kernel(per_tile, taps_ref, frames_ref, before_ref, after_ref, *refs):
+    out_ref = refs[-1]
+    steps = frames_ref.shape[0]
+    taps = [taps_ref[j] for j in range(2 * REACH + 1)]
+
+    def body(tile, carry):
+        for group in range(per_tile // SUBLANES):
+            at = pl.multiple_of(tile * per_tile + group * SUBLANES, SUBLANES)
+            rows = pl.ds(at, SUBLANES)
+            field = [before_ref[t, rows, :] for t in range(REACH)]
+            field += [frames_ref[t, 0, rows, :] for t in range(steps)]
+            field += [after_ref[t, rows, :] for t in range(REACH)]
+            inside = pl.ds(group * SUBLANES, SUBLANES)
+            for t in range(steps):
+                out_ref[tile, 0, t, inside, :] = weighted(taps, field, t)
+        return carry
+
+    lax.fori_loop(0, out_ref.shape[0], body, 0)
+
+
+def early_chunk(taps, frames, before, after, packed, shape, start, offset):
+    steps, _, strip, columns = frames.shape
+    tile_rows, groups, _, per_tile, _ = shape
+    span = columns // groups
+    width = before.shape[2] // groups
+    per_group = width // LANES
+    side = pl.BlockSpec((REACH, strip, LANES), lambda g, i: (0, 0, g * per_group + i))
+    in_specs = [
+        pl.BlockSpec(memory_space=pltpu.SMEM),
+        pl.BlockSpec(
+            (steps, 1, strip, LANES),
+            lambda g, i: (0, 0, 0, g * (span // LANES) + start // LANES + i),
+        ),
+        side,
+        side,
+    ]
+    operands = [taps, frames, before, after]
+    aliases = {}
+    if packed is not None:
+        in_specs.append(pl.BlockSpec(memory_space=pl.ANY))
+        aliases = {len(operands): 0}
+        operands.append(packed)
+    elements = strip * groups * width
+    return pl.pallas_call(
+        functools.partial(early_kernel, per_tile),
+        grid=(groups, per_group),
+        out_shape=jax.ShapeDtypeStruct(shape, jnp.float32),
+        in_specs=in_specs,
+        out_specs=pl.BlockSpec(
+            (tile_rows, 1, steps, per_tile, LANES),
+            lambda g, i: (0, g, 0, 0, offset // LANES + i),
+        ),
+        input_output_aliases=aliases,
+        cost_estimate=pl.CostEstimate(
+            flops=14 * steps * elements,
+            bytes_accessed=4 * (2 * steps + 2 * REACH) * elements,
+            transcendentals=0,
+        ),
+        name="early",
+    )(*operands)
+
+
+def place_kernel(readers, groups, piece_ref, *refs):
+    out_ref = refs[-1]
+
+    def body(group, carry):
+        rows = pl.ds(pl.multiple_of(group * SUBLANES, SUBLANES), SUBLANES)
+        for s in range(readers):
+            at = group * (SUBLANES * readers) + s
+            for t in range(out_ref.shape[1]):
+                out_ref[0, t, pl.ds(at, SUBLANES, stride=readers), :] = piece_ref[s, t, rows, :]
+        return carry
+
+    lax.fori_loop(0, groups, body, 0)
 
 
 def pack_kernel(per_tile, frames_ref, first_ref, middle_ref, last_ref):
@@ -94,18 +212,15 @@
                 after_mid[s, 1, rows, :],
             ]
             for t in range(steps):
-                total = taps[0] * field[t]
-                for j in range(1, 2 * REACH + 1):
-                    total = total + taps[j] * field[t + j]
                 at = group * (SUBLANES * readers) + s
-                out_ref[0, t, pl.ds(at, SUBLANES, stride=readers), :] = total
+                out_ref[0, t, pl.ds(at, SUBLANES, stride=readers), :] = weighted(taps, field, t)
         return carry
 
     lax.fori_loop(0, groups, body, 0)
 
 
-def smooth_chunk(taps, pieces, out, out_shape, start, width):
-    readers, _, per_tile, _ = pieces[0].shape
+def write_tiles(kernel, scalars, pieces, out, out_shape, start, flops):
+    readers, _, per_tile, width = pieces[0].shape
     steps = out_shape[1]
     offset = start // LANES
     per_row = TS // LANES
@@ -115,16 +230,18 @@
             (readers, piece.shape[1], per_tile, LANES), lambda i: (0, 0, 0, i)
         )
 
-    in_specs = [pl.BlockSpec(memory_space=pltpu.SMEM)] + [piece_spec(p) for p in pieces]
-    operands = [taps, *pieces]
+    in_specs = [pl.BlockSpec(memory_space=pltpu.SMEM) for _ in scalars]
+    in_specs += [piece_spec(p) for p in pieces]
+    operands = [*scalars, *pieces]
     aliases = {}
     if out is not None:
         in_specs.append(pl.BlockSpec(memory_space=pl.ANY))
         aliases = {len(operands): 0}
         operands.append(out)
     elements = readers * per_tile * width
+    moved = steps + sum(p.shape[1] for p in pieces)
     return pl.pallas_call(
-        functools.partial(smooth_kernel, readers, per_tile // SUBLANES),
+        functools.partial(kernel, readers, per_tile // SUBLANES),
         grid=(width // LANES,),
         out_shape=jax.ShapeDtypeStruct(out_shape, jnp.float32),
         in_specs=in_specs,
@@ -134,10 +251,8 @@
         ),
         input_output_aliases=aliases,
         cost_estimate=pl.CostEstimate(
-            flops=14 * steps * elements, bytes_accessed=14 * 4 * elements, transcendentals=0
-        ),
-        compiler_params=pltpu.CompilerParams(dimension_semantics=("arbitrary",)),
-        name="smooth",
+            flops=flops * steps * elements, bytes_accessed=4 * moved * elements, transcendentals=0
+        ),
     )(*operands)
 
 
@@ -149,15 +264,24 @@
     tile_rows = strip // per_tile
     owned = tile_rows * (columns // TS) // readers
     span = owned * TS
+    groups = columns // span
     out_shape = (owned, steps, TS, TS)
     up = [(i, i + 1) for i in range(count - 1)]
     down = [(i + 1, i) for i in range(count - 1)]
     swap = functools.partial(
         lax.all_to_all, axis_name="sa", split_axis=0, concat_axis=0, tiled=True
     )
-
-    out = None
-    for start, stop in chunk_bounds(span):
+    early, late = chunk_bounds(span)
+
+    sides = []
+    for start, stop in early:
+        tail, head = raw_chunk(frames, span, start, stop - start)
+        before = lax.ppermute(tail, "ta", up)
+        after = lax.ppermute(head, "ta", down)
+        sides.append((before, after))
+
+    exchanged = []
+    for start, stop in late:
         first, middle, last = pack_chunk(frames, readers, per_tile, span, start, stop - start)
         middle = swap(middle)
         before_mid = lax.ppermute(middle, "ta", up)
@@ -166,8 +290,23 @@
         after_first = lax.ppermute(first, "ta", down)
         last = swap(last)
         before_last = lax.ppermute(last, "ta", up)
-        pieces = (first, middle, last, before_mid, before_last, after_first, after_mid)
-        out = smooth_chunk(taps, pieces, out, out_shape, start, stop - start)
+        exchanged.append(
+            (first, middle, last, before_mid, before_last, after_first, after_mid)
+        )
+
+    out = None
+    if early:
+        packed = None
+        width = early[-1][1] - early[0][0]
+        shape = (tile_rows, groups, steps, per_tile, width)
+        for (start, stop), (before, after) in zip(early, sides):
+            packed = early_chunk(
+                taps, frames, before, after, packed, shape, start, start - early[0][0]
+            )
+        packed = swap(packed.reshape(readers, steps, per_tile, width))
+        out = write_tiles(place_kernel, (), (packed,), None, out_shape, early[0][0], 1)
+    for (start, stop), pieces in zip(late, exchanged):
+        out = write_tiles(smooth_kernel, (taps,), pieces, out, out_shape, start, 14)
     return out
 
 

time: 966 us -> 706 us (0.73)
  blocking collectives: 264 us -> 99.2 us
  starting transfers between devices: 145 us -> 55.3 us
    ppermute x8 -> x2, waiting for transfers between devices: 197 us -> 0.01 us  [on_device(): before_mid = lax.ppermute(middle, 'ta', up)]
    ppermute x8 -> x2, waiting for transfers between devices: 84.5 us -> 278 us  [on_device(): before_last = lax.ppermute(last, 'ta', up)]
    all_to_all x7 -> x2, blocking collectives: 143 us -> 79.7 us  [on_device(): last = swap(last)]
    ppermute x0 -> x4, waiting for transfers between devices: none -> 60 us  [the longest x2 54.2 us: on_device(): before = lax.ppermute(tail, 'ta', up)]
    all_to_all x2 -> x0, blocking collectives: 59.6 us -> none  [on_device(): middle = swap(middle)]
    all_to_all x6 -> x2, waiting for transfers between devices: 45.7 us -> 99.6 us  [on_device(): middle = swap(middle)]
    all_to_all x3 -> x1, blocking collectives: 62.3 us -> 19.6 us  [on_device(): first = swap(first)]
    all_to_all x5 -> x1, waiting for transfers between devices: 40 us -> 0.01 us  [on_device(): first = swap(first)]
  transfers between devices with their start and end apart: 44 -> 16, of which waited for: 25 -> 8; matrix products, arithmetic and copies ran while one was open for 0% -> 0% of each run, Pallas kernels for 9% -> 12%
where the time goes in v2:
time: 706 us; the launch traced here: 705 us
  waiting for transfers between devices  449 us (64%)
  blocking collectives  99.2 us (14%)
  Pallas kernels  97.6 us (14%)
  starting transfers between devices  55.3 us (8%)
    ppermute x2, waiting for transfers between devices, on_device(): before_last = lax.ppermute(last, 'ta', up)  278 us
    all_to_all x2, waiting for transfers between devices, on_device(): middle = swap(middle)  99.6 us
    all_to_all x2, blocking collectives, on_device(): last = swap(last)  79.7 us
    ppermute x2, waiting for transfers between devices, on_device(): before = lax.ppermute(tail, 'ta', up)  54.2 us
    pallas_call x3, Pallas kernels, write_tiles(): pl.pallas_call(functools.partial(kernel, readers, per_tile // SUBLANES),...  47.8 us
    pallas_call x2, Pallas kernels, pack_chunk(): pl.pallas_call(functools.partial(pack_kernel, per_tile), grid=(groups, wi...  20.9 us
    all_to_all x1, blocking collectives, on_device(): first = swap(first)  19.6 us
    pallas_call x2, Pallas kernels, early_chunk(): pl.pallas_call(functools.partial(early_kernel, per_tile), grid=(groups, p...  17.2 us
  transfers between devices with their start and end apart: 16, of which 8 were waited for; matrix products, arithmetic and copies ran while one was open for 0% of the time, Pallas kernels for 12%

profile of v2, /device:TPU:0, one launch (start us, length us, event | category | flops | bytes accessed | tf_op | source)
XLA Modules:
  0.0 704.6 jit_solution(15513750562674045448)
XLA Ops:
  0.0 4.4 pack.2
  4.4 20.5 %all_to_all.35.refs_2_ = f32[8,1,64,512]{3,2,1,0:T(8,128)S(1)} all-to-all(f32[8,1,64,512]{3,2,1,0:T(8,128)} %bitcast.13), channel_id=1, replica_groups=mesh['ta'=4,'sa'=8] {'sa'}, dimensions={0} | all-to-all | bytes 2097152 | tf_op jit(solution)/shard_map/all_to_all | solution.py:291
  24.9 0.0 copy-start.3
  24.9 19.6 %all_to_all.36.refs_0_ = f32[8,1,64,512]{3,2,1,0:T(8,128)} all-to-all(f32[8,1,64,512]{3,2,1,0:T(8,128)} %bitcast.12), channel_id=1, replica_groups=mesh['ta'=4,'sa'=8] {'sa'}, dimensions={0} | all-to-all | bytes 2097152 | tf_op jit(solution)/shard_map/all_to_all | solution.py:289
  44.5 3.6 all-to-all-start.1
  48.1 16.5 %pack.3 = (f32[8,1,1,64,2304]{4,3,2,1,0:T(8,128)}, f32[8,1,2,64,2304]{4,3,2,1,0:T(8,128)}, f32[8,1,1,64,2304]{4,3,2,1,0:T(8,128)}) custom-call(f32[4,1,512,4096]{3,2,1,0:T(8,128)} %frames_ref.11), custom_call_target="tpu_custom_call" | custom-call | flops 4718592 | bytes 37748736 | tf_op jit(solution)/shard_map/pack/pallas_call | solution.py:172
  64.6 10.0 %all-to-all-done.1.refs_1_ = f32[8,2,64,512]{3,2,1,0:T(8,128)S(1)} async-done(((f32[8,2,64,512]{3,2,1,0:T(8,128)}), f32[8,2,64,512]{3,2,1,0:T(8,128)S(1)}, u32[]{:S(2)}, u32[]{:S(2)}) %all-to-all-start.1) | async-done | bytes 2097184 | tf_op jit(solution)/shard_map/all_to_all | solution.py:286
  74.6 0.0 copy-start
  74.6 59.2 %all_to_all.37.refs_2_ = f32[8,1,64,2304]{3,2,1,0:T(8,128)} all-to-all(f32[8,1,64,2304]{3,2,1,0:T(8,128)} %bitcast.10), channel_id=1, replica_groups=mesh['ta'=4,'sa'=8] {'sa'}, dimensions={0} | all-to-all | bytes 9437184 | tf_op jit(solution)/shard_map/all_to_all | solution.py:291
  133.8 5.0 all-to-all-start.4
  138.8 8.3 %raw.2 = (f32[3,512,1024]{2,1,0:T(8,128)}, f32[3,512,1024]{2,1,0:T(8,128)}) custom-call(f32[4,1,512,4096]{3,2,1,0:T(8,128)} %frames_ref.11), custom_call_target="tpu_custom_call" | custom-call | flops 524288 | bytes 20971520 | tf_op jit(solution)/shard_map/raw/pallas_call | solution.py:51
  147.1 6.2 collective-permute-start.8
  153.2 1.3 collective-permute-start.9
  154.5 89.6 %all-to-all-done.4.refs_1_ = f32[8,2,64,2304]{3,2,1,0:T(8,128)} async-done(((f32[8,2,64,2304]{3,2,1,0:T(8,128)}), f32[8,2,64,2304]{3,2,1,0:T(8,128)}, u32[]{:S(2)}, u32[]{:S(2)}) %all-to-all-start.4) | async-done | bytes 9437216 | tf_op jit(solution)/shard_map/all_to_all | solution.py:286
  244.1 4.6 all-to-all-start.3
  248.7 3.5 raw.3
  252.1 4.6 collective-permute-start.10
  256.8 1.3 collective-permute-start.11
  258.0 8.2 %collective-permute-start.4 = (f32[8,2,64,2304]{3,2,1,0:T(8,128)}, f32[8,2,64,2304]{3,2,1,0:T(8,128)}, u32[]{:S(2)}, u32[]{:S(2)}) collective-permute-start(f32[8,2,64,2304]{3,2,1,0:T(8,128)} %all-to-all-done.4.refs_1_), channel_id=1, source_target_pairs={{0,8},{8,16},{16,24},{1,9},{9,17},{17,25},{2,10},{10,18},{18,26},{... | collective-permute-start | bytes 28311560 | tf_op jit(solution)/shard_map/ppermute | solution.py:287
  266.2 54.2 %collective-permute-done.10.before_ref = f32[3,512,256]{2,1,0:T(8,128)} collective-permute-done((f32[3,512,256]{2,1,0:T(8,128)}, f32[3,512,256]{2,1,0:T(8,128)}, u32[]{:S(2)}, u32[]{:S(2)}) %collective-permute-start.10) | collective-permute-done | bytes 1572896 | tf_op jit(solution)/shard_map/ppermute | solution.py:279
  320.5 1.3 collective-permute-start.7
  321.7 5.8 collective-permute-done.11.after_ref
  327.5 4.0 early.2.refs_0_
  331.5 0.0 collective-permute-done.8.before_ref
  331.5 0.0 collective-permute-done.9.after_ref
  331.5 13.2 %early.3 = f32[8,1,4,64,1280]{4,3,2,1,0:T(8,128)} custom-call(f32[7]{0:T(128)} %taps_ref.7, f32[4,1,512,4096]{3,2,1,0:T(8,128)} %frames_ref.11, f32[3,512,1024]{2,1,0:T(8,128)} %collective-permute-done.8.before_ref, f32[3,512,1024]{2,1,0:T(8,128)} %collective-permute-done.9.after_ref, ...), custom_call_target="tpu_custom_call", output_to_operand_aliasing={{}: (4, {})} | custom-call | flops 29360128 | bytes 29360128 | tf_op jit(solution)/shard_map/early/pallas_call | solution.py:115
  344.7 0.0 all-to-all-done.3.refs_0_
  344.8 5.1 all-to-all-start.6
  349.9 1.8 collective-permute-start.5
  351.7 1.3 collective-permute-start.6
  353.0 5.9 collective-permute-start
  358.9 264.9 %collective-permute-done.5.refs_4_ = f32[8,1,64,2304]{3,2,1,0:T(8,128)S(1)} collective-permute-done((f32[8,1,64,2304]{3,2,1,0:T(8,128)}, f32[8,1,64,2304]{3,2,1,0:T(8,128)S(1)}, u32[]{:S(2)}, u32[]{:S(2)}) %collective-permute-start.5) | collective-permute-done | bytes 4718624 | tf_op jit(solution)/shard_map/ppermute | solution.py:292
  623.8 0.0 copy-done
  623.8 0.0 copy-start.1
  623.8 1.3 collective-permute-start.3
  625.1 0.8 copy-done.1
  625.9 4.9 collective-permute-done.6.refs_5_
  630.8 0.0 copy-done.3
  630.8 0.0 copy-start.2
  630.8 2.1 copy-done.2
  632.9 2.6 collective-permute-start.1
  635.5 0.0 collective-permute-done.4.refs_3_
  635.5 1.3 collective-permute-start.2
  636.8 0.0 all-to-all-done.6.piece_ref
  636.8 11.8 %shard_map.28.refs_7_ = f32[8,4,512,512]{3,2,1,0:T(8,128)} custom-call(f32[8,4,64,1280]{3,2,1,0:T(8,128)} %all-to-all-done.6.piece_ref), custom_call_target="tpu_custom_call" | custom-call | flops 2621440 | bytes 20971520 | tf_op jit(solution)/shard_map/pallas_call | solution.py:243
  648.6 0.0 collective-permute-done.7.refs_6_
  648.6 28.8 %shard_map.29.refs_7_ = f32[8,4,512,512]{3,2,1,0:T(8,128)} custom-call(f32[7]{0:T(128)} %taps_ref.7, f32[8,1,64,2304]{3,2,1,0:T(8,128)} %all-to-all-done.3.refs_0_, f32[8,2,64,2304]{3,2,1,0:T(8,128)} %all-to-all-done.4.refs_1_, f32[8,1,64,2304]{3,2,1,0:T(8,128)} %all_to_all.37.refs_2_, ...), custom_call_target="tpu_custom_call", output_to_operand_aliasing={{}: (8, {})} | custom-call | flops 66060288 | bytes 66060288 | tf_op jit(solution)/shard_map/pallas_call | solution.py:243
  677.4 13.1 %collective-permute-done.1.refs_4_ = f32[8,1,64,512]{3,2,1,0:T(8,128)} collective-permute-done((f32[8,1,64,512]{3,2,1,0:T(8,128)S(1)}, f32[8,1,64,512]{3,2,1,0:T(8,128)}, u32[]{:S(2)}, u32[]{:S(2)}) %collective-permute-start.1) | collective-permute-done | bytes 1048608 | tf_op jit(solution)/shard_map/ppermute | solution.py:292
  690.5 6.9 collective-permute-done.2.refs_5_
  697.4 0.0 collective-permute-done.refs_3_
  697.4 0.0 collective-permute-done.3.refs_6_
  697.4 7.2 %shard_map.30 = f32[8,4,512,512]{3,2,1,0:T(8,128)} custom-call(f32[7]{0:T(128)} %taps_ref.7, f32[8,1,64,512]{3,2,1,0:T(8,128)} %all_to_all.36.refs_0_, f32[8,2,64,512]{3,2,1,0:T(8,128)} %copy-done, f32[8,1,64,512]{3,2,1,0:T(8,128)} %copy-done.3, f32[8,2,64,512]{3,2,1,0:T(8,128)} %collective-permute-done.refs_3_, ...), custom_call_target="tpu_custom_call", output_to_operand_aliasing={{}: (8, {})} | custom-call | flops 14680064 | bytes 14680064 | tf_op jit(solution)/shard_map/pallas_call | solution.py:243
Async XLA Ops:
  24.9 605.9 %copy-start.3 = (f32[8,1,64,512]{3,2,1,0:T(8,128)}, f32[8,1,64,512]{3,2,1,0:T(8,128)S(1)}, u32[]{:S(2)}) copy-start(f32[8,1,64,512]{3,2,1,0:T(8,128)S(1)} %all_to_all.35.refs_2_) | copy-start | bytes 3145732
  44.5 30.2 %all-to-all-start.1 = ((f32[8,2,64,512]{3,2,1,0:T(8,128)}), f32[8,2,64,512]{3,2,1,0:T(8,128)S(1)}, u32[]{:S(2)}, u32[]{:S(2)}) async-start(f32[8,2,64,512]{3,2,1,0:T(8,128)} %bitcast.11), calls=%async_computation.1 | async-start | bytes 4194304 | tf_op jit(solution)/shard_map/all_to_all | solution.py:286
  74.6 549.2 %copy-start = (f32[8,2,64,512]{3,2,1,0:T(8,128)}, f32[8,2,64,512]{3,2,1,0:T(8,128)S(1)}, u32[]{:S(2)}) copy-start(f32[8,2,64,512]{3,2,1,0:T(8,128)S(1)} %all-to-all-done.1.refs_1_) | copy-start | bytes 6291460
  133.8 110.3 %all-to-all-start.4 = ((f32[8,2,64,2304]{3,2,1,0:T(8,128)}), f32[8,2,64,2304]{3,2,1,0:T(8,128)}, u32[]{:S(2)}, u32[]{:S(2)}) async-start(f32[8,2,64,2304]{3,2,1,0:T(8,128)} %bitcast.8), calls=%async_computation.4 | async-start | bytes 18874368 | tf_op jit(solution)/shard_map/all_to_all | solution.py:286
  147.1 184.5 %collective-permute-start.8 = (f32[3,512,1024]{2,1,0:T(8,128)}, f32[3,512,1024]{2,1,0:T(8,128)}, u32[]{:S(2)}, u32[]{:S(2)}) collective-permute-start(f32[3,512,1024]{2,1,0:T(8,128)} %get-tuple-element.21), channel_id=1, source_target_pairs={{0,8},{8,16},{16,24},{1,9},{9,17},{17,25},{2,10},{10,18},{18,26},{... | collective-permute-start | bytes 18874376 | tf_op jit(solution)/shard_map/ppermute | solution.py:279
  153.2 178.3 %collective-permute-start.9 = (f32[3,512,1024]{2,1,0:T(8,128)}, f32[3,512,1024]{2,1,0:T(8,128)}, u32[]{:S(2)}, u32[]{:S(2)}) collective-permute-start(f32[3,512,1024]{2,1,0:T(8,128)} %get-tuple-element.22), channel_id=1, source_target_pairs={{8,0},{16,8},{24,16},{9,1},{17,9},{25,17},{10,2},{18,10},{26,18},{... | collective-permute-start | bytes 18874376 | tf_op jit(solution)/shard_map/ppermute | solution.py:280
  244.1 100.7 %all-to-all-start.3 = ((f32[8,1,64,2304]{3,2,1,0:T(8,128)}), f32[8,1,64,2304]{3,2,1,0:T(8,128)}, u32[]{:S(2)}, u32[]{:S(2)}) async-start(f32[8,1,64,2304]{3,2,1,0:T(8,128)} %bitcast.9), calls=%async_computation.3 | async-start | bytes 9437184 | tf_op jit(solution)/shard_map/all_to_all | solution.py:289
  252.1 68.3 %collective-permute-start.10 = (f32[3,512,256]{2,1,0:T(8,128)}, f32[3,512,256]{2,1,0:T(8,128)}, u32[]{:S(2)}, u32[]{:S(2)}) collective-permute-start(f32[3,512,256]{2,1,0:T(8,128)} %get-tuple-element.23), channel_id=1, source_target_pairs={{0,8},{8,16},{16,24},{1,9},{9,17},{17,25},{2,10},{10,18},{18,26},{... | collective-permute-start | bytes 4718600 | tf_op jit(solution)/shard_map/ppermute | solution.py:279
  256.8 70.8 %collective-permute-start.11 = (f32[3,512,256]{2,1,0:T(8,128)}, f32[3,512,256]{2,1,0:T(8,128)}, u32[]{:S(2)}, u32[]{:S(2)}) collective-permute-start(f32[3,512,256]{2,1,0:T(8,128)} %get-tuple-element.24), channel_id=1, source_target_pairs={{8,0},{16,8},{24,16},{9,1},{17,9},{25,17},{10,2},{18,10},{26,18},{... | collective-permute-start | bytes 4718600 | tf_op jit(solution)/shard_map/ppermute | solution.py:280
  258.0 377.4 %collective-permute-start.4 = (f32[8,2,64,2304]{3,2,1,0:T(8,128)}, f32[8,2,64,2304]{3,2,1,0:T(8,128)}, u32[]{:S(2)}, u32[]{:S(2)}) collective-permute-start(f32[8,2,64,2304]{3,2,1,0:T(8,128)} %all-to-all-done.4.refs_1_), channel_id=1, source_target_pairs={{0,8},{8,16},{16,24},{1,9},{9,17},{17,25},{2,10},{10,18},{18,26},{... | collective-permute-start | bytes 28311560 | tf_op jit(solution)/shard_map/ppermute | solution.py:287
  320.5 328.1 %collective-permute-start.7 = (f32[8,2,64,2304]{3,2,1,0:T(8,128)}, f32[8,2,64,2304]{3,2,1,0:T(8,128)}, u32[]{:S(2)}, u32[]{:S(2)}) collective-permute-start(f32[8,2,64,2304]{3,2,1,0:T(8,128)} %all-to-all-done.4.refs_1_), channel_id=1, source_target_pairs={{8,0},{16,8},{24,16},{9,1},{17,9},{25,17},{10,2},{18,10},{26,18},{... | collective-permute-start | bytes 28311560 | tf_op jit(solution)/shard_map/ppermute | solution.py:288
  344.8 292.0 %all-to-all-start.6 = ((f32[8,4,64,1280]{3,2,1,0:T(8,128)}), f32[8,4,64,1280]{3,2,1,0:T(8,128)}, u32[]{:S(2)}, u32[]{:S(2)}) async-start(f32[8,4,64,1280]{3,2,1,0:T(8,128)} %bitcast.7), calls=%async_computation.6 | async-start | bytes 20971520 | tf_op jit(solution)/shard_map/all_to_all | solution.py:306
  349.9 273.9 %collective-permute-start.5 = (f32[8,1,64,2304]{3,2,1,0:T(8,128)}, f32[8,1,64,2304]{3,2,1,0:T(8,128)S(1)}, u32[]{:S(2)}, u32[]{:S(2)}) collective-permute-start(f32[8,1,64,2304]{3,2,1,0:T(8,128)} %all_to_all.37.refs_2_), channel_id=1, source_target_pairs={{0,8},{8,16},{16,24},{1,9},{9,17},{17,25},{2,10},{10,18},{18,26},{... | collective-permute-start | bytes 14155784 | tf_op jit(solution)/shard_map/ppermute | solution.py:292
  351.7 279.1 %collective-permute-start.6 = (f32[8,1,64,2304]{3,2,1,0:T(8,128)}, f32[8,1,64,2304]{3,2,1,0:T(8,128)S(1)}, u32[]{:S(2)}, u32[]{:S(2)}) collective-permute-start(f32[8,1,64,2304]{3,2,1,0:T(8,128)} %all-to-all-done.3.refs_0_), channel_id=1, source_target_pairs={{8,0},{16,8},{24,16},{9,1},{17,9},{25,17},{10,2},{18,10},{26,18},{... | collective-permute-start | bytes 14155784 | tf_op jit(solution)/shard_map/ppermute | solution.py:290
  353.0 344.5 %collective-permute-start = (f32[8,2,64,512]{3,2,1,0:T(8,128)S(1)}, f32[8,2,64,512]{3,2,1,0:T(8,128)}, u32[]{:S(2)}, u32[]{:S(2)}) collective-permute-start(f32[8,2,64,512]{3,2,1,0:T(8,128)S(1)} %all-to-all-done.1.refs_1_), channel_id=1, source_target_pairs={{0,8},{8,16},{16,24},{1,9},{9,17},{17,25},{2,10},{10,18},{18,26},{... | collective-permute-start | bytes 6291464 | tf_op jit(solution)/shard_map/ppermute | solution.py:287
  623.8 2.1 copy-start.1
  623.8 73.6 %collective-permute-start.3 = (f32[8,2,64,512]{3,2,1,0:T(8,128)S(1)}, f32[8,2,64,512]{3,2,1,0:T(8,128)}, u32[]{:S(2)}, u32[]{:S(2)}) collective-permute-start(f32[8,2,64,512]{3,2,1,0:T(8,128)S(1)} %all-to-all-done.1.refs_1_), channel_id=1, source_target_pairs={{8,0},{16,8},{24,16},{9,1},{17,9},{25,17},{10,2},{18,10},{26,18},{... | collective-permute-start | bytes 6291464 | tf_op jit(solution)/shard_map/ppermute | solution.py:288
  630.8 2.1 copy-start.2
  632.9 57.6 %collective-permute-start.1 = (f32[8,1,64,512]{3,2,1,0:T(8,128)S(1)}, f32[8,1,64,512]{3,2,1,0:T(8,128)}, u32[]{:S(2)}, u32[]{:S(2)}) collective-permute-start(f32[8,1,64,512]{3,2,1,0:T(8,128)S(1)} %all_to_all.35.refs_2_), channel_id=1, source_target_pairs={{0,8},{8,16},{16,24},{1,9},{9,17},{17,25},{2,10},{10,18},{18,26},{... | collective-permute-start | bytes 3145736 | tf_op jit(solution)/shard_map/ppermute | solution.py:292
  635.5 62.0 %collective-permute-start.2 = (f32[8,1,64,512]{3,2,1,0:T(8,128)}, f32[8,1,64,512]{3,2,1,0:T(8,128)}, u32[]{:S(2)}, u32[]{:S(2)}) collective-permute-start(f32[8,1,64,512]{3,2,1,0:T(8,128)} %all_to_all.36.refs_0_), channel_id=1, source_target_pairs={{8,0},{16,8},{24,16},{9,1},{17,9},{25,17},{10,2},{18,10},{26,18},{... | collective-permute-start | bytes 3145736 | tf_op jit(solution)/shard_map/ppermute | solution.py:290
